TPU v7x, 512 devices: a whole 4x4x16 slice. The times are simulated.
512 devices in a mesh: psg: 128 (over z, x, core), head: 4 (over y).
Axes of the slice: x: 4, y: 4, z: 16, core: 2. Of those that a mesh axis runs over, the one named last changes fastest.
Arguments:
- queries: bfloat16 [1024, 2048], P('psg', 'head'), may hold values from -16 to 16
- passage_keys: bfloat16 [256, 256, 2048], P('psg', None, 'head'), may hold values from -6 to 6
- passage_values: bfloat16 [256, 256, 2048], P('psg', None, 'head'), may hold values from -6 to 6
- shelf_ids: int32 [1024, 16], P('psg'), may hold values from 0 to 127, all different within a row; in each aligned block of 8 rows (0 to 7, 8 to 15, ...) at most 2 rows name the same one
- live_mask: int32 [1024, 32], P('psg'), may hold values 0 or 1
- w_out: bfloat16 [2048, 2048], P('head'), may hold values from -0.75 to 0.75
Outputs:
- out: bfloat16 [1024, 2048], P('psg', 'head')
Inputs may be any that keep to these rules, and one draw needn't show every extreme that they name: `shelf_ids`: each row names 16 different shelves. Among the rows of one device, no shelf is named by more than 2 rows, and in some devices one shelf is named by exactly 2 rows.
All inputs are finite; a program needn't handle non-finite values. No bound on the sum of `live_mask` on one device may be relied on, other than what follows from the above.
Results may differ from a plain program's by a relative error of at most 0.0085.
Values may be sent and summed in bfloat16 or wider, within the bound.
No kernel may reach another device: no remote copies, remote signals or barrier semaphores. Data moves between devices by JAX's collectives and lax.ppermute only.
A program may use at most 64 MiB of HBM per device.

v0:
```python
import jax
import jax.numpy as jnp
from jax import lax
from jax.sharding import PartitionSpec as P

DK = 64


far_below = -1e30


def sent_together(arrays, axis, split_dim, concat_dim, along):
    both = jnp.concatenate(arrays, axis=along)
    result, at, finished = (
        lax.all_to_all(both, axis, split_axis=split_dim, concat_axis=concat_dim, tiled=True),
        0,
        [],
    )
    for a in arrays:
        finished.append(lax.slice_in_dim(result, at, at + a.shape[along], axis=along))
        at += a.shape[along]
    return tuple(finished)


def cut_along(x, dim, length):
    before, after = (x.shape[:dim], x.shape[dim + 1 :])
    return jnp.moveaxis(x.reshape(*before, length, -1, *after), dim, 0)


def summed_on_arrival(x, axis, dim):
    length = lax.axis_size(axis)
    blocks = lax.all_to_all(cut_along(x, dim, length), axis, 0, 0, tiled=True)
    return jnp.sum(blocks, axis=0)


def shelf_partials(query_rows, live_bits, passage_keys, passage_values):
    row_count = query_rows.shape[0]
    heads_here = query_rows.shape[1] // DK
    passages_here = passage_keys.shape[0]
    length = passage_keys.shape[1]
    query_heads = query_rows.reshape(row_count, heads_here, DK).transpose(1, 0, 2)
    key_heads = passage_keys.reshape(passages_here * length, heads_here, DK).transpose(1, 0, 2)
    value_heads = passage_values.reshape(passages_here * length, heads_here, DK).transpose(1, 0, 2)
    key_live = jnp.repeat(live_bits > 0, length, axis=1)

    def one_head(operands):
        query_head, key_head, value_head = operands
        scores = jnp.dot(query_head, key_head.T, preferred_element_type=jnp.float32)
        scores = jnp.where(key_live, scores, far_below)
        peak_score = jnp.max(scores, axis=1)
        exp_scores = jnp.exp(scores - peak_score[:, None])
        exp_total = jnp.sum(exp_scores, axis=1)
        weights = exp_scores.astype(jnp.bfloat16)
        context = (
            jnp.dot(weights, value_head, preferred_element_type=jnp.float32) / exp_total[:, None]
        )
        return (context, peak_score, exp_total)

    context, peak_score, exp_total = lax.map(one_head, (query_heads, key_heads, value_heads))
    return (
        context.transpose(1, 0, 2).reshape(row_count, heads_here * DK),
        peak_score.T,
        exp_total.T,
    )


def merge_shelves(context, peak_score, exp_total, has_live):
    request_count, shelf_count, heads_here = peak_score.shape
    masked_peak = jnp.where(has_live[:, :, None], peak_score, far_below)
    best_peak = jnp.max(masked_peak, axis=1)
    shelf_share = jnp.where(
        has_live[:, :, None], exp_total * jnp.exp(masked_peak - best_peak[:, None, :]), 0.0
    )
    context_heads = context.reshape(request_count, shelf_count, heads_here, DK)
    attended = (
        jnp.sum(shelf_share[:, :, :, None] * context_heads, axis=1)
        / jnp.sum(shelf_share, axis=1)[:, :, None]
    )
    return attended.reshape(request_count, heads_here * DK).astype(jnp.bfloat16)


def per_device(queries, passage_keys, passage_values, shelf_ids, live_mask, w_out):
    owners = lax.axis_size("psg")
    requests_here, shelves = shelf_ids.shape
    passages_here = passage_keys.shape[0]
    hidden_width = queries.shape[1]
    capacity = max(2, min(requests_here, 2 * requests_here * shelves // owners))
    first_entry = (jnp.arange(live_mask.shape[1], dtype=jnp.int32) == 0).astype(jnp.int32)
    live_bits = jnp.maximum(live_mask, first_entry[None, :]).reshape(
        requests_here, shelves, passages_here
    )
    owner_ids = jnp.arange(owners, dtype=jnp.int32)
    presence = jnp.sum(
        (shelf_ids[:, :, None] == owner_ids[None, None, :]).astype(jnp.int32), axis=1
    )
    rank_table = jnp.cumsum(presence, axis=0) - presence
    slot_index = jnp.take_along_axis(rank_table, shelf_ids, axis=1)
    box_index = (shelf_ids * capacity + slot_index).reshape(-1)
    repeated = jnp.broadcast_to(
        queries[:, None, :], (requests_here, shelves, hidden_width)
    ).reshape(-1, hidden_width)
    query_box = (
        jnp.zeros((owners * capacity, hidden_width), jnp.bfloat16).at[box_index].set(repeated)
    )
    query_box = query_box.reshape(owners, capacity, hidden_width)
    live_box = (
        jnp.zeros((owners * capacity, passages_here), jnp.int32)
        .at[box_index]
        .set(live_bits.reshape(-1, passages_here))
    )
    live_box = live_box.reshape(owners, capacity, passages_here)
    got_queries, got_live = (
        lax.all_to_all(query_box, "psg", split_axis=0, concat_axis=0, tiled=True),
        lax.all_to_all(live_box, "psg", split_axis=0, concat_axis=0, tiled=True),
    )
    senders = got_queries.shape[0]
    slots_here = got_queries.shape[1]
    context, peak_score, exp_total = shelf_partials(
        got_queries.reshape(senders * slots_here, hidden_width),
        got_live.reshape(senders * slots_here, passages_here),
        passage_keys,
        passage_values,
    )
    heads_here = peak_score.shape[1]
    context, peak_score, exp_total = sent_together(
        (
            context.reshape(senders, slots_here, hidden_width),
            peak_score.reshape(senders, slots_here, heads_here),
            exp_total.reshape(senders, slots_here, heads_here),
        ),
        "psg",
        0,
        0,
        2,
    )
    heads_here = peak_score.shape[2]
    context = context.reshape(owners * capacity, hidden_width)[box_index].reshape(
        requests_here, shelves, hidden_width
    )
    peak_score = peak_score.reshape(owners * capacity, heads_here)[box_index].reshape(
        requests_here, shelves, heads_here
    )
    exp_total = exp_total.reshape(owners * capacity, heads_here)[box_index].reshape(
        requests_here, shelves, heads_here
    )
    has_live = jnp.max(live_bits, axis=2) > 0
    attended = merge_shelves(context, peak_score, exp_total, has_live)
    projected = jnp.dot(attended, w_out, preferred_element_type=jnp.float32)
    return summed_on_arrival(projected, "head", 1).astype(jnp.bfloat16)


def solution(mesh):
    in_specs = (
        P("psg", "head"),
        P("psg", None, "head"),
        P("psg", None, "head"),
        P("psg", None),
        P("psg", None),
        P("head", None),
    )
    out_specs = P("psg", "head")
    return jax.shard_map(
        per_device, mesh=mesh, in_specs=in_specs, out_specs=out_specs, check_vma=False
    )
```

profile of v0, /device:TPU:32, one launch (start us, length us, event | category | flops | bytes accessed | tf_op | source)
XLA Modules:
  0.0 142.5 jit_solution(4157931596576514944)
XLA Ops:
  0.0 0.8 convert_reduce_fusion
  0.8 0.7 bitcast_or_fusion
  1.6 1.0 gather_fusion.3
  2.9 0.9 scatter_custom_fusion.1
  3.8 1.5 %copy.84 = s32[128,2,2]{1,2,0:T(2,128)} copy(s32[128,2,2]{2,1,0:T(2,128)S(1)} %bitcast.79) | data formatting | bytes 4096 | tf_op jit(solution)/shard_map/reshape | solution.py:111
  5.3 19.0 %all-to-all-start.1 = ((s32[128,2,2]{1,2,0:T(2,128)}), s32[128,2,2]{1,2,0:T(2,128)S(1)}, u32[]{:S(2)}, u32[]{:S(2)}) async-start(s32[128,2,2]{1,2,0:T(2,128)} %copy.84), calls=%async_computation.1 | async-start | bytes 262144 | tf_op jit(solution)/shard_map/all_to_all | solution.py:114
  24.4 1.1 scatter_custom_fusion
  25.5 0.8 reshape.131
  26.3 15.1 %all-to-all-done.1 = s32[128,2,2]{1,2,0:T(2,128)S(1)} async-done(((s32[128,2,2]{1,2,0:T(2,128)}), s32[128,2,2]{1,2,0:T(2,128)S(1)}, u32[]{:S(2)}, u32[]{:S(2)}) %all-to-all-start.1) | async-done | bytes 2080 | tf_op jit(solution)/shard_map/all_to_all | solution.py:114
  41.4 6.1 %all-to-all-start = ((bf16[128,2,512]{2,1,0:T(2,128)(2,1)}), bf16[128,2,512]{2,1,0:T(2,128)(2,1)S(1)}, u32[]{:S(2)}, u32[]{:S(2)}) async-start(bf16[128,2,512]{2,1,0:T(2,128)(2,1)} %reshape.131), calls=%async_computation | async-start | bytes 524288 | tf_op jit(solution)/shard_map/all_to_all | solution.py:113
  47.6 0.5 copy.81
  49.6 20.4 %all-to-all-done = bf16[128,2,512]{2,1,0:T(2,128)(2,1)S(1)} async-done(((bf16[128,2,512]{2,1,0:T(2,128)(2,1)}), bf16[128,2,512]{2,1,0:T(2,128)(2,1)S(1)}, u32[]{:S(2)}, u32[]{:S(2)}) %all-to-all-start) | async-done | bytes 262176 | tf_op jit(solution)/shard_map/all_to_all | solution.py:113
  70.5 9.5 %while.15 = (s32[]{:T(128)}, f32[8,256,64]{1,2,0:T(8,128)S(1)}, f32[8,256]{1,0:T(8,128)S(1)}, f32[8,256]{1,0:T(8,128)S(1)}, bf16[8,256,64]{2,1,0:T(8,128)(2,1)S(...) while((s32[]{:T(128)}, f32[8,256,64]{1,2,0:T(8,128)S(1)}, ...), condition=%wide.region_8.9_spmd.clone, body=%wide.region_5.8_spmd.clone.sunk | while | flops 34356736 | bytes 2371181 | solution.py:59
  81.1 1.2 pad_maximum_fusion
  82.3 6.3 %all-to-all-start.2 = ((f32[128,2,528]{2,1,0:T(2,128)}), f32[128,2,528]{2,1,0:T(2,128)S(1)}, u32[]{:S(2)}, u32[]{:S(2)}) async-start(f32[128,2,528]{2,1,0:T(2,128)} %pad_maximum_fusion), calls=%async_computation.2 | async-start | bytes 1310720 | tf_op jit(solution)/shard_map/all_to_all | solution.py:15
  88.7 2.9 %copy.96 = bf16[2048,512]{1,0:T(8,128)(2,1)S(1)} copy(bf16[2048,512]{0,1:T(8,128)(2,1)} %bitcast.74) | data formatting | bytes 4194304 | tf_op jit(solution)/shard_map/dot_general | solution.py:148
  91.6 35.7 %all-to-all-done.2 = f32[128,2,528]{2,1,0:T(2,128)S(1)} async-done(((f32[128,2,528]{2,1,0:T(2,128)}), f32[128,2,528]{2,1,0:T(2,128)S(1)}, u32[]{:S(2)}, u32[]{:S(2)}) %all-to-all-start.2) | async-done | bytes 540704 | tf_op jit(solution)/shard_map/all_to_all | solution.py:15
  127.5 0.6 gather_fusion
  128.2 0.6 gather_fusion.1
  129.2 0.8 gather_fusion.2
  130.1 0.9 fusion.32
  131.4 0.6 convolution_bitcast_fusion
  132.0 9.9 %all_to_all.20 = f32[4,8,512]{2,1,0:T(8,128)S(1)} all-to-all(f32[4,8,512]{2,1,0:T(8,128)S(1)} %convolution_bitcast_fusion), channel_id=1, replica_groups=mesh['psg'=128,'head'=4] {'head'}, dimensions={0} | all-to-all | bytes 131072 | tf_op jit(solution)/shard_map/all_to_all | solution.py:32
  141.9 0.6 reduce_sum.48
  (105 shorter events, 13.9 us)
Async XLA Ops:
  1.6 1.1 copy-start.2
  1.6 1.2 copy-start.4
  1.6 22.8 %copy-start.3 = (bf16[8,512]{1,0:T(8,128)(2,1)S(1)}, bf16[8,512]{1,0:T(8,128)(2,1)}, u32[]{:S(2)}) copy-start(bf16[8,512]{1,0:T(8,128)(2,1)} %param.8) | copy-start | bytes 24580
  2.6 45.0 %copy-start = (bf16[2,256,512]{2,1,0:T(8,128)(2,1)S(1)}, bf16[2,256,512]{2,1,0:T(8,128)(2,1)}, u32[]{:S(2)}) copy-start(bf16[2,256,512]{2,1,0:T(8,128)(2,1)} %param.9) | copy-start | bytes 1572868
  2.9 45.5 %copy-start.1 = (bf16[2,256,512]{2,1,0:T(8,128)(2,1)S(1)}, bf16[2,256,512]{2,1,0:T(8,128)(2,1)}, u32[]{:S(2)}) copy-start(bf16[2,256,512]{2,1,0:T(8,128)(2,1)} %param.10) | copy-start | bytes 1572868
  5.3 36.1 %all-to-all-start.1 = ((s32[128,2,2]{1,2,0:T(2,128)}), s32[128,2,2]{1,2,0:T(2,128)S(1)}, u32[]{:S(2)}, u32[]{:S(2)}) async-start(s32[128,2,2]{1,2,0:T(2,128)} %copy.84), calls=%async_computation.1 | async-start | bytes 262144 | tf_op jit(solution)/shard_map/all_to_all | solution.py:114
  41.4 28.6 %all-to-all-start = ((bf16[128,2,512]{2,1,0:T(2,128)(2,1)}), bf16[128,2,512]{2,1,0:T(2,128)(2,1)S(1)}, u32[]{:S(2)}, u32[]{:S(2)}) async-start(bf16[128,2,512]{2,1,0:T(2,128)(2,1)} %reshape.131), calls=%async_computation | async-start | bytes 524288 | tf_op jit(solution)/shard_map/all_to_all | solution.py:113
  82.3 45.1 %all-to-all-start.2 = ((f32[128,2,528]{2,1,0:T(2,128)}), f32[128,2,528]{2,1,0:T(2,128)S(1)}, u32[]{:S(2)}, u32[]{:S(2)}) async-start(f32[128,2,528]{2,1,0:T(2,128)} %pad_maximum_fusion), calls=%async_computation.2 | async-start | bytes 1310720 | tf_op jit(solution)/shard_map/all_to_all | solution.py:15
where the time goes:
time: 143 us
  waiting for transfers between devices  71.3 us (50%)
  starting transfers between devices  31.4 us (22%)
  local copies, waits for them, and re-layouts  17.7 us (12%)
  blocking collectives  9.89 us (7%)
  other arithmetic  6.39 us (4%)
  matrix products  5.29 us (4%)
    all_to_all x1, waiting for transfers between devices, sent_together(): lax.all_to_all(both, axis, split_axis=split_dim, concat_axis=concat_dim,...  35.7 us
    all_to_all x1, waiting for transfers between devices, per_device(): lax.all_to_all(query_box, 'psg', split_axis=0, concat_axis=0, tiled=True)  20.4 us
    all_to_all x1, starting transfers between devices, per_device(): lax.all_to_all(live_box, 'psg', split_axis=0, concat_axis=0, tiled=True)  19 us
    all_to_all x1, waiting for transfers between devices, per_device(): lax.all_to_all(live_box, 'psg', split_axis=0, concat_axis=0, tiled=True)  15.1 us
    all_to_all x1, blocking collectives, summed_on_arrival(): blocks = lax.all_to_all(cut_along(x, dim, length), axis, 0, 0, tiled=True)  9.89 us
    all_to_all x1, starting transfers between devices, sent_together(): lax.all_to_all(both, axis, split_axis=split_dim, concat_axis=concat_dim,...  6.26 us
    all_to_all x1, starting transfers between devices, per_device(): lax.all_to_all(query_box, 'psg', split_axis=0, concat_axis=0, tiled=True)  6.1 us
    dot_general x1, local copies, waits for them, and re-layouts, per_device(): projected = jnp.dot(attended, w_out, preferred_element_type=jnp.float32)  2.86 us
  transfers between devices with their start and end apart: 3, of which 3 were waited for; matrix products, arithmetic and copies ran while one was open for 5% of the time, Pallas kernels for 0%

commit v1 on v0

v1 whole, which is shorter than its diff:
```python
import jax
import jax.numpy as jnp
from jax import lax
from jax.experimental import pallas as pl
from jax.experimental.pallas import tpu as pltpu
from jax.sharding import PartitionSpec as P

DK = 64
SLOTS = 2
LANES = 128
far_below = -1e30
bf16 = jnp.bfloat16
f32 = jnp.float32


def first_member(owners):
    return owners // 2 + owners // 32 + 1 if owners >= 32 else 0


def rotated_group(owners):
    first = first_member(owners)
    return [[(first + i) % owners for i in range(owners)]]


def dot(a, b, dims):
    return lax.dot_general(a, b, (dims, ((), ())), preferred_element_type=f32)


def choose(shelf_ids, live_mask, owners):
    requests, shelves = shelf_ids.shape
    columns = owners * SLOTS
    column = lax.broadcasted_iota(jnp.int32, (requests, columns), 1)
    position = column // SLOTS + first_member(owners)
    owner = jnp.where(position >= owners, position - owners, position)
    present = jnp.zeros((requests, columns), f32)
    live0 = jnp.zeros((requests, columns), f32)
    live1 = jnp.zeros((requests, columns), f32)
    for j in range(shelves):
        hit = (shelf_ids[:, j : j + 1] == owner).astype(f32)
        present = present + hit
        first = live_mask[:, 2 * j : 2 * j + 1].astype(f32)
        first = jnp.ones_like(first) if j == 0 else first
        live0 = live0 + hit * first
        live1 = live1 + hit * live_mask[:, 2 * j + 1 : 2 * j + 2].astype(f32)
    rank = jnp.zeros((1, columns), f32)
    ranks = []
    for r in range(requests):
        ranks.append(rank)
        rank = rank + present[r : r + 1]
    rank = jnp.concatenate(ranks, axis=0)
    slot = (column % SLOTS).astype(f32)
    mine = jnp.where(rank == slot, present, 0.0)
    return mine, mine * live0, mine * live1


def box_kernel(queries, shelf_ids, live_mask, box):
    requests, width = queries.shape
    owners = box.shape[0]
    mine, live0, live1 = choose(shelf_ids[...], live_mask[...], owners)
    dead0 = live1 * (1.0 - live0)
    dead1 = live0 * (1.0 - live1)
    lane = lax.broadcasted_iota(jnp.int32, (requests, LANES), 1)
    rows = dot(mine.astype(bf16), queries[...], ((0,), (0,)))
    flags = dot(
        jnp.concatenate([dead0, dead1], axis=0).astype(bf16),
        jnp.concatenate([(lane == 0).astype(f32), (lane == 1).astype(f32)], axis=0).astype(bf16),
        ((0,), (0,)),
    )
    both = jnp.concatenate([rows, flags], axis=1).astype(bf16)
    box[...] = both.reshape(box.shape)


def shelf_kernel(box, keys, values, out):
    senders, slots, wide = box.shape
    rows = senders * slots
    width = wide - LANES
    passages, length, _ = keys.shape
    positions = passages * length
    got = box[...].reshape(rows, wide)
    flags = got[:, width:]
    key_rows = keys[...].reshape(positions, width)
    value_rows = values[...].reshape(positions, width)
    place = lax.broadcasted_iota(jnp.int32, (positions, LANES), 0) // length
    lane = lax.broadcasted_iota(jnp.int32, (positions, LANES), 1)
    bias = jnp.where(place == lane, far_below, 0.0).astype(bf16)
    ones = jnp.ones((positions, LANES), bf16)
    stat_lane = lax.broadcasted_iota(jnp.int32, (rows, LANES), 1)
    low = stat_lane < DK
    keep = [jnp.where(low, 1.0, 0.0).astype(bf16), jnp.where(low, 0.0, 1.0).astype(bf16)]
    heads = width // DK
    stats = jnp.zeros((rows, LANES), f32)
    contexts = []
    for pair in range(width // LANES):
        at = pair * LANES
        query_pair = got[:, at : at + LANES]
        key_pair = jnp.concatenate([key_rows[:, at : at + LANES], bias], axis=1)
        value_pair = jnp.concatenate([value_rows[:, at : at + LANES], ones], axis=1)
        halves = []
        for half in range(2):
            query = query_pair * keep[half]
            scores = dot(jnp.concatenate([query, flags], axis=1), key_pair, ((1,), (1,)))
            peak = jnp.max(scores, axis=1, keepdims=True).astype(bf16).astype(f32)
            weights = jnp.exp(scores - peak).astype(bf16)
            summed = dot(weights, value_pair, ((1,), (0,)))
            total = summed[:, LANES:]
            halves.append(summed[:, :LANES] / total)
            high = total.astype(bf16).astype(f32)
            head = 2 * pair + half
            stats = jnp.where(stat_lane == head, peak, stats)
            stats = jnp.where(stat_lane == heads + head, high, stats)
            stats = jnp.where(stat_lane == 2 * heads + head, total - high, stats)
        contexts.append(jnp.where(low, halves[0], halves[1]).astype(bf16))
    both = jnp.concatenate(contexts + [stats.astype(bf16)], axis=1)
    out[...] = both.reshape(out.shape)


def merge_kernel(box, shelf_ids, live_mask, w_out, out):
    owners, slots, wide = box.shape
    rows = owners * slots
    width = wide - LANES
    heads = width // DK
    requests = shelf_ids.shape[0]
    mine, live0, live1 = choose(shelf_ids[...], live_mask[...], owners)
    read = (live0 + live1) > 0.0
    got = box[...].reshape(rows, wide)
    stats = got[:, width:].astype(f32).T
    shares = []
    totals = []
    for h in range(heads):
        peak = jnp.where(read, stats[h : h + 1], far_below)
        best = jnp.max(peak, axis=1, keepdims=True)
        total = stats[heads + h : heads + h + 1] + stats[2 * heads + h : 2 * heads + h + 1]
        share = jnp.where(read, total * jnp.exp(peak - best), 0.0)
        shares.append(share)
        totals.append(jnp.sum(share, axis=1, keepdims=True))
    share = jnp.concatenate(shares, axis=0)
    high = share.astype(bf16)
    rest = (share - high.astype(f32)).astype(bf16)
    context = got[:, :width]
    summed = dot(high, context, ((1,), (0,))) + dot(rest, context, ((1,), (0,)))
    head_of = lax.broadcasted_iota(jnp.int32, (requests, width), 1) // DK
    attended = jnp.zeros((requests, width), f32)
    for h in range(heads):
        part = summed[h * requests : (h + 1) * requests] / totals[h]
        attended = jnp.where(head_of == h, part, attended)
    attended = attended.astype(bf16)
    groups, _, columns = out.shape
    for g in range(groups):
        out[g] = dot(attended, w_out[:, g * columns : (g + 1) * columns], ((1,), (0,)))


def vmem(n):
    return [pl.BlockSpec(memory_space=pltpu.VMEM)] * n


def per_device(queries, passage_keys, passage_values, shelf_ids, live_mask, w_out):
    owners = lax.axis_size("psg")
    groups = lax.axis_size("head")
    requests, width = queries.shape
    wide = width + LANES
    box_shape = jax.ShapeDtypeStruct((owners, SLOTS, wide), bf16)
    out_spec = pl.BlockSpec(memory_space=pltpu.VMEM)

    def exchanged(x):
        return lax.all_to_all(
            x, "psg", split_axis=0, concat_axis=0, axis_index_groups=rotated_group(owners), tiled=True
        )

    box = pl.pallas_call(
        box_kernel, out_shape=box_shape, in_specs=vmem(3), out_specs=out_spec, name="box"
    )(queries, shelf_ids, live_mask)
    partials = pl.pallas_call(
        shelf_kernel, out_shape=box_shape, in_specs=vmem(3), out_specs=out_spec, name="shelf"
    )(exchanged(box), passage_keys, passage_values)
    projected = pl.pallas_call(
        merge_kernel,
        out_shape=jax.ShapeDtypeStruct((groups, requests, w_out.shape[1] // groups), f32),
        in_specs=vmem(4),
        out_specs=out_spec,
        name="merge",
    )(exchanged(partials), shelf_ids, live_mask, w_out)
    blocks = lax.all_to_all(projected, "head", 0, 0, tiled=True)
    return jnp.sum(blocks, axis=0).astype(bf16)


def solution(mesh):
    in_specs = (
        P("psg", "head"),
        P("psg", None, "head"),
        P("psg", None, "head"),
        P("psg", None),
        P("psg", None),
        P("head", None),
    )
    out_specs = P("psg", "head")
    return jax.shard_map(
        per_device, mesh=mesh, in_specs=in_specs, out_specs=out_specs, check_vma=False
    )
```

time: 143 us -> 90.5 us (0.63)
  the two profiles are of different devices: /device:TPU:32 before, /device:TPU:4 now
where the time goes in v1:
time: 90.5 us; the launch traced here: 90.1 us
  blocking collectives  80.5 us (89%)
  Pallas kernels  9 us (10%)
    all_to_all x2, blocking collectives, exchanged(): lax.all_to_all(x, 'psg', split_axis=0, concat_axis=0, axis_index_groups=r...  70.4 us
    all_to_all x1, blocking collectives, per_device(): blocks = lax.all_to_all(projected, 'head', 0, 0, tiled=True)  10.1 us
    pallas_call x1, Pallas kernels, per_device(): pl.pallas_call(shelf_kernel, out_shape=box_shape, in_specs=vmem(3), out_s...  3.94 us
    pallas_call x1, Pallas kernels, per_device(): pl.pallas_call(merge_kernel, out_shape=jax.ShapeDtypeStruct((groups, requ...  3.16 us
    pallas_call x1, Pallas kernels, per_device(): pl.pallas_call(box_kernel, out_shape=box_shape, in_specs=vmem(3), out_spe...  1.91 us

profile of v1, /device:TPU:4, one launch (start us, length us, event | category | flops | bytes accessed | tf_op | source)
XLA Modules:
  0.0 90.1 jit_solution(14239410422070992103)
XLA Ops:
  0.0 1.9 %box.1 = bf16[128,2,640]{2,1,0:T(2,128)(2,1)} custom-call(bf16[8,512]{1,0:T(8,128)(2,1)} %queries.1, s32[8,16]{1,0:T(8,128)} %shelf_ids.3, s32[8,32]{1,0:T(8,128)} %live_mask.3), custom_call_target="tpu_custom_call" | custom-call | tf_op jit(solution)/shard_map/box/pallas_call | solution.py:169
  1.9 38.4 %all_to_all.15.box = bf16[128,2,640]{2,1,0:T(2,128)(2,1)} all-to-all(bf16[128,2,640]{2,1,0:T(2,128)(2,1)} %box.1), channel_id=1, replica_groups={{276,280,284,288,292,296,300,304,308,312,316,320,324,328,332,336,340,34..., dimensions={0} | all-to-all | bytes 655360 | tf_op jit(solution)/shard_map/all_to_all | solution.py:165
  40.3 3.9 %shelf.1 = bf16[128,2,640]{2,1,0:T(2,128)(2,1)} custom-call(bf16[128,2,640]{2,1,0:T(2,128)(2,1)} %all_to_all.15.box, bf16[2,256,512]{2,1,0:T(8,128)(2,1)} %keys.1, bf16[2,256,512]{2,1,0:T(8,128)(2,1)} %values.1), custom_call_target="tpu_custom_call" | custom-call | tf_op jit(solution)/shard_map/shelf/pallas_call | solution.py:172
  44.2 32.0 %all_to_all.16.box = bf16[128,2,640]{2,1,0:T(2,128)(2,1)} all-to-all(bf16[128,2,640]{2,1,0:T(2,128)(2,1)} %shelf.1), channel_id=1, replica_groups={{276,280,284,288,292,296,300,304,308,312,316,320,324,328,332,336,340,34..., dimensions={0} | all-to-all | bytes 655360 | tf_op jit(solution)/shard_map/all_to_all | solution.py:165
  76.2 3.2 %merge.1 = f32[4,8,512]{2,1,0:T(8,128)} custom-call(bf16[128,2,640]{2,1,0:T(2,128)(2,1)} %all_to_all.16.box, s32[8,16]{1,0:T(8,128)} %shelf_ids.3, s32[8,32]{1,0:T(8,128)} %live_mask.3, bf16[512,2048]{1,0:T(8,128)(2,1)} %w_out.1), custom_call_target="tpu_custom_call" | custom-call | tf_op jit(solution)/shard_map/merge/pallas_call | solution.py:175
  79.4 10.1 %all_to_all.17 = f32[4,8,512]{2,1,0:T(8,128)S(1)} all-to-all(f32[4,8,512]{2,1,0:T(8,128)} %merge.1), channel_id=1, replica_groups=mesh['psg'=128,'head'=4] {'head'}, dimensions={0} | all-to-all | bytes 131072 | tf_op jit(solution)/shard_map/all_to_all | solution.py:182
  89.5 0.6 reduce_sum.9

commit v2 on v1

--- a/solution.py
+++ b/solution.py
@@ -8,6 +8,7 @@
 DK = 64
 SLOTS = 2
 LANES = 128
+KERNEL_VMEM = 24 << 20
 far_below = -1e30
 bf16 = jnp.bfloat16
 f32 = jnp.float32
@@ -149,8 +150,45 @@
         out[g] = dot(attended, w_out[:, g * columns : (g + 1) * columns], ((1,), (0,)))
 
 
-def vmem(n):
-    return [pl.BlockSpec(memory_space=pltpu.VMEM)] * n
+def stage_kernel(*refs):
+    count = (len(refs) - 1) // 2
+    copies = [
+        pltpu.make_async_copy(refs[n], refs[count + n], refs[-1].at[n]) for n in range(count)
+    ]
+    for copy in copies:
+        copy.start()
+    for copy in copies:
+        copy.wait()
+
+
+def in_vmem(shape, dtype):
+    return pltpu.VMEM(shape, dtype)
+
+
+def staged(*arrays):
+    return pl.pallas_call(
+        stage_kernel,
+        out_shape=[in_vmem(a.shape, a.dtype) for a in arrays],
+        in_specs=[pl.BlockSpec(memory_space=pl.ANY)] * len(arrays),
+        out_specs=[pl.BlockSpec(memory_space=pltpu.VMEM)] * len(arrays),
+        scratch_shapes=[pltpu.SemaphoreType.DMA((len(arrays),))],
+        compiler_params=pltpu.CompilerParams(vmem_limit_bytes=1 << 20),
+        name="stage",
+    )(*[pltpu.with_memory_space_constraint(a, pltpu.HBM) for a in arrays])
+
+
+def call(kernel, shape, dtype, name, near, far=()):
+    spec = pl.BlockSpec(memory_space=pltpu.VMEM)
+    near = [pltpu.with_memory_space_constraint(a, pltpu.VMEM) for a in near]
+    far = [pltpu.with_memory_space_constraint(a, pltpu.HBM) for a in far]
+    return pl.pallas_call(
+        kernel,
+        out_shape=in_vmem(shape, dtype),
+        in_specs=[spec] * (len(near) + len(far)),
+        out_specs=spec,
+        compiler_params=pltpu.CompilerParams(vmem_limit_bytes=KERNEL_VMEM),
+        name=name,
+    )(*near, *far)
 
 
 def per_device(queries, passage_keys, passage_values, shelf_ids, live_mask, w_out):
@@ -158,27 +196,24 @@
     groups = lax.axis_size("head")
     requests, width = queries.shape
     wide = width + LANES
-    box_shape = jax.ShapeDtypeStruct((owners, SLOTS, wide), bf16)
-    out_spec = pl.BlockSpec(memory_space=pltpu.VMEM)
-
     def exchanged(x):
         return lax.all_to_all(
             x, "psg", split_axis=0, concat_axis=0, axis_index_groups=rotated_group(owners), tiled=True
         )
 
-    box = pl.pallas_call(
-        box_kernel, out_shape=box_shape, in_specs=vmem(3), out_specs=out_spec, name="box"
-    )(queries, shelf_ids, live_mask)
-    partials = pl.pallas_call(
-        shelf_kernel, out_shape=box_shape, in_specs=vmem(3), out_specs=out_spec, name="shelf"
-    )(exchanged(box), passage_keys, passage_values)
-    projected = pl.pallas_call(
+    box_shape = (owners, SLOTS, wide)
+    box = call(box_kernel, box_shape, bf16, "box", (), (queries, shelf_ids, live_mask))
+    keys, values, w_near, ids_near, live_near = staged(
+        passage_keys, passage_values, w_out, shelf_ids, live_mask
+    )
+    partials = call(shelf_kernel, box_shape, bf16, "shelf", (exchanged(box), keys, values))
+    projected = call(
         merge_kernel,
-        out_shape=jax.ShapeDtypeStruct((groups, requests, w_out.shape[1] // groups), f32),
-        in_specs=vmem(4),
-        out_specs=out_spec,
-        name="merge",
-    )(exchanged(partials), shelf_ids, live_mask, w_out)
+        (groups, requests, w_out.shape[1] // groups),
+        f32,
+        "merge",
+        (exchanged(partials), ids_near, live_near, w_near),
+    )
     blocks = lax.all_to_all(projected, "head", 0, 0, tiled=True)
     return jnp.sum(blocks, axis=0).astype(bf16)
 

time: 90.5 us -> 84.5 us (0.934)
  blocking collectives: 80.5 us -> 40.7 us
  starting transfers between devices: 0 us -> 20.8 us
  waiting for transfers between devices: 0 us -> 15.5 us
  Pallas kernels: 9 us -> 6.59 us
    all_to_all x2 -> x1, blocking collectives: 70.4 us -> 30.8 us  [exchanged(): lax.all_to_all(x, 'psg', split_axis=0, concat_axis=0, axis_index_groups=r...]
    all_to_all x0 -> x1, starting transfers between devices: none -> 20.8 us  [exchanged(): lax.all_to_all(x, 'psg', split_axis=0, concat_axis=0, axis_index_groups=r...]
    all_to_all x0 -> x1, waiting for transfers between devices: none -> 15.5 us  [exchanged(): lax.all_to_all(x, 'psg', split_axis=0, concat_axis=0, axis_index_groups=r...]
    pallas_call x3 -> x4, Pallas kernels: 9 us -> 6.59 us  [the longest x3 4.61 us: call(): pl.pallas_call(kernel, out_shape=in_vmem(shape, dtype), in_specs=[spec] *...]
  transfers between devices with their start and end apart: 0 -> 1, of which waited for: 0 -> 1; matrix products, arithmetic and copies ran while one was open for 0% -> 0% of each run, Pallas kernels for 0% -> 2%
where the time goes in v2:
time: 84.5 us; the launch traced here: 84.3 us
  blocking collectives  40.7 us (48%)
  starting transfers between devices  20.8 us (25%)
  waiting for transfers between devices  15.5 us (18%)
  Pallas kernels  6.59 us (8%)
    all_to_all x1, blocking collectives, exchanged(): lax.all_to_all(x, 'psg', split_axis=0, concat_axis=0, axis_index_groups=r...  30.8 us
    all_to_all x1, starting transfers between devices, exchanged(): lax.all_to_all(x, 'psg', split_axis=0, concat_axis=0, axis_index_groups=r...  20.8 us
    all_to_all x1, waiting for transfers between devices, exchanged(): lax.all_to_all(x, 'psg', split_axis=0, concat_axis=0, axis_index_groups=r...  15.5 us
    all_to_all x1, blocking collectives, per_device(): blocks = lax.all_to_all(projected, 'head', 0, 0, tiled=True)  9.89 us
    pallas_call x3, Pallas kernels, call(): pl.pallas_call(kernel, out_shape=in_vmem(shape, dtype), in_specs=[spec] *...  4.61 us
    pallas_call x1, Pallas kernels, staged(): pl.pallas_call(stage_kernel, out_shape=[in_vmem(a.shape, a.dtype) for a i...  1.98 us
  transfers between devices with their start and end apart: 1, of which 1 were waited for; matrix products, arithmetic and copies ran while one was open for 0% of the time, Pallas kernels for 2%

profile of v2, /device:TPU:4, one launch (start us, length us, event | category | flops | bytes accessed | tf_op | source)
XLA Modules:
  0.0 84.3 jit_solution(9149078213914019752)
XLA Ops:
  0.0 1.9 %box.1 = bf16[128,2,640]{2,1,0:T(2,128)(2,1)} custom-call(bf16[8,512]{1,0:T(8,128)(2,1)} %queries.1, s32[8,16]{1,0:T(8,128)} %refs_3_.1, s32[8,32]{1,0:T(8,128)} %refs_4_.1), custom_call_target="tpu_custom_call" | custom-call | tf_op jit(solution)/shard_map/box/pallas_call | solution.py:184
  1.9 20.8 %all-to-all-start = ((bf16[128,2,640]{2,1,0:T(2,128)(2,1)}), bf16[128,2,640]{2,1,0:T(2,128)(2,1)S(1)}, u32[]{:S(2)}, u32[]{:S(2)}) async-start(bf16[128,2,640]{2,1,0:T(2,128)(2,1)} %box.1), calls=%async_computation | async-start | bytes 655360 | tf_op jit(solution)/shard_map/all_to_all | solution.py:200
  22.7 2.0 %stage.1 = (bf16[2,256,512]{2,1,0:T(8,128)(2,1)S(1)}, bf16[2,256,512]{2,1,0:T(8,128)(2,1)S(1)}, bf16[512,2048]{1,0:T(8,128)(2,1)S(1)}, s32[8,16]{1,0:T(8,128)S(1)}, s32[8,32]{1,0:T(8,128)S(1)}) custom-call(bf16[2,256,512]{2,1,0:T(8,128)(2,1)} %refs_0_.1, bf16[2,256,512]{2,1,0:T(8,128)(2,1)} %refs_1_.1, bf16[512,2048]{1,0:T(8,128)(2,1)} %refs_2_.1, ...), custom_call_target="tpu_custom_call" | custom-call | tf_op jit(solution)/shard_map/stage/pallas_call | solution.py:169
  24.7 15.5 %all-to-all-done.box = bf16[128,2,640]{2,1,0:T(2,128)(2,1)S(1)} async-done(((bf16[128,2,640]{2,1,0:T(2,128)(2,1)}), bf16[128,2,640]{2,1,0:T(2,128)(2,1)S(1)}, u32[]{:S(2)}, u32[]{:S(2)}) %all-to-all-start) | async-done | bytes 327712 | tf_op jit(solution)/shard_map/all_to_all | solution.py:200
  40.2 1.9 %shelf.1 = bf16[128,2,640]{2,1,0:T(2,128)(2,1)S(1)} custom-call(bf16[128,2,640]{2,1,0:T(2,128)(2,1)S(1)} %all-to-all-done.box, bf16[2,256,512]{2,1,0:T(8,128)(2,1)S(1)} %get-tuple-element.10.keys, bf16[2,256,512]{2,1,0:T(8,128)(2,1)S(1)} %get-tuple-element.11.values), custom_call_target="tpu_custom_call" | custom-call | tf_op jit(solution)/shard_map/shelf/pallas_call | solution.py:184
  42.1 30.8 %all_to_all.15.box = bf16[128,2,640]{2,1,0:T(2,128)(2,1)S(1)} all-to-all(bf16[128,2,640]{2,1,0:T(2,128)(2,1)S(1)} %shelf.1), channel_id=1, replica_groups={{276,280,284,288,292,296,300,304,308,312,316,320,324,328,332,336,340,34..., dimensions={0} | all-to-all | bytes 655360 | tf_op jit(solution)/shard_map/all_to_all | solution.py:200
  73.0 0.8 merge.1
  73.8 9.9 %all_to_all.16 = f32[4,8,512]{2,1,0:T(8,128)S(1)} all-to-all(f32[4,8,512]{2,1,0:T(8,128)S(1)} %merge.1), channel_id=1, replica_groups=mesh['psg'=128,'head'=4] {'head'}, dimensions={0} | all-to-all | bytes 131072 | tf_op jit(solution)/shard_map/all_to_all | solution.py:217
  83.7 0.6 reduce_sum.9
Async XLA Ops:
  1.9 38.3 %all-to-all-start = ((bf16[128,2,640]{2,1,0:T(2,128)(2,1)}), bf16[128,2,640]{2,1,0:T(2,128)(2,1)S(1)}, u32[]{:S(2)}, u32[]{:S(2)}) async-start(bf16[128,2,640]{2,1,0:T(2,128)(2,1)} %box.1), calls=%async_computation | async-start | bytes 655360 | tf_op jit(solution)/shard_map/all_to_all | solution.py:200

commit v3 on v2

v3 whole, which is shorter than its diff:
```python
import jax
import jax.numpy as jnp
from jax import lax
from jax.experimental import pallas as pl
from jax.experimental.pallas import tpu as pltpu
from jax.sharding import PartitionSpec as P

DK = 64
SLOTS = 2
CORES = 2
LANES = 128
KERNEL_VMEM = 24 << 20
far_below = -1e30
bf16 = jnp.bfloat16
f32 = jnp.float32


def first_chip(chips):
    return chips // 2 + chips // 32 if chips >= 32 else 0


def rotated(length, first):
    return [(first + i) % length for i in range(length)]


def same_core_groups(owners):
    chips = owners // CORES
    order = rotated(chips, first_chip(chips))
    return [[CORES * chip + core for chip in order] for core in range(CORES)]


def dot(a, b, dims):
    return lax.dot_general(a, b, (dims, ((), ())), preferred_element_type=f32)


def own_core():
    return lax.axis_index("psg") % CORES


def choose(shelf_ids, live_mask, chips, core):
    requests, shelves = shelf_ids.shape
    half = chips * SLOTS
    columns = CORES * half
    column = lax.broadcasted_iota(jnp.int32, (requests, columns), 1)
    other = (column >= half).astype(jnp.int32)
    place = (column - other * half) // SLOTS + first_chip(chips)
    chip = jnp.where(place >= chips, place - chips, place)
    owner = CORES * chip + jnp.where(other == core, 0, 1)
    present = jnp.zeros((requests, columns), f32)
    live0 = jnp.zeros((requests, columns), f32)
    live1 = jnp.zeros((requests, columns), f32)
    for j in range(shelves):
        hit = (shelf_ids[:, j : j + 1] == owner).astype(f32)
        present = present + hit
        first = live_mask[:, 2 * j : 2 * j + 1].astype(f32)
        first = jnp.ones_like(first) if j == 0 else first
        live0 = live0 + hit * first
        live1 = live1 + hit * live_mask[:, 2 * j + 1 : 2 * j + 2].astype(f32)
    rank = jnp.zeros((1, columns), f32)
    ranks = []
    for r in range(requests):
        ranks.append(rank)
        rank = rank + present[r : r + 1]
    rank = jnp.concatenate(ranks, axis=0)
    slot = (column % SLOTS).astype(f32)
    mine = jnp.where(rank == slot, present, 0.0)
    return mine, mine * live0, mine * live1


def box_kernel(queries, shelf_ids, live_mask, box):
    requests, width = queries.shape
    chips = box.shape[0]
    half = chips * SLOTS
    mine, live0, live1 = choose(shelf_ids[...], live_mask[...], chips, own_core())
    dead0 = live1 * (1.0 - live0)
    dead1 = live0 * (1.0 - live1)
    dead = [dead0[:, :half], dead1[:, :half], dead0[:, half:], dead1[:, half:]]
    lane = lax.broadcasted_iota(jnp.int32, (requests, LANES), 1)
    rows = dot(mine.astype(bf16), queries[...], ((0,), (0,)))
    flags = dot(
        jnp.concatenate(dead, axis=0).astype(bf16),
        jnp.concatenate([(lane == n).astype(f32) for n in range(len(dead))], axis=0).astype(bf16),
        ((0,), (0,)),
    )
    both = jnp.concatenate([rows[:half], rows[half:], flags], axis=1).astype(bf16)
    box[...] = both.reshape(box.shape)


def shelf_kernel(box, keys, values, other_keys, other_values, out):
    chips, slots, wide = box.shape
    rows = chips * slots
    width = (wide - LANES) // CORES
    passages, length, _ = keys.shape
    positions = passages * length
    heads = width // DK
    got = box[...].reshape(rows, wide)
    flags = got[:, CORES * width :]
    flags = jnp.concatenate([flags, flags], axis=0)
    place = lax.broadcasted_iota(jnp.int32, (positions, LANES), 0) // length
    lane = lax.broadcasted_iota(jnp.int32, (positions, LANES), 1)
    ones = jnp.ones((positions, LANES), bf16)
    stat_lane = lax.broadcasted_iota(jnp.int32, (rows, LANES), 1)
    low = stat_lane < DK
    keep = [jnp.where(low, 1.0, 0.0).astype(bf16), jnp.where(low, 0.0, 1.0).astype(bf16)]
    stats = jnp.zeros((rows, LANES), f32)
    contexts = []
    for shelf, (key_ref, value_ref) in enumerate(((keys, values), (other_keys, other_values))):
        bias = jnp.where(place + passages * shelf == lane, far_below, 0.0).astype(bf16)
        key_rows = key_ref[...].reshape(positions, width)
        value_rows = value_ref[...].reshape(positions, width)
        for pair in range(width // LANES):
            at = pair * LANES
            query_pair = got[:, shelf * width + at : shelf * width + at + LANES]
            query = jnp.concatenate([query_pair * keep[0], query_pair * keep[1]], axis=0)
            key_pair = jnp.concatenate([key_rows[:, at : at + LANES], bias], axis=1)
            value_pair = jnp.concatenate([value_rows[:, at : at + LANES], ones], axis=1)
            scores = dot(jnp.concatenate([query, flags], axis=1), key_pair, ((1,), (1,)))
            peak = jnp.max(scores, axis=1, keepdims=True).astype(bf16).astype(f32)
            weights = jnp.exp(scores - peak).astype(bf16)
            summed = dot(weights, value_pair, ((1,), (0,)))
            total = summed[:, LANES:]
            context = summed[:, :LANES] / total
            contexts.append(jnp.where(low, context[:rows], context[rows:]).astype(bf16))
            high = total.astype(bf16).astype(f32)
            for part in range(2):
                own = slice(part * rows, (part + 1) * rows)
                at_lane = 3 * heads * shelf + 2 * pair + part
                stats = jnp.where(stat_lane == at_lane, peak[own], stats)
                stats = jnp.where(stat_lane == at_lane + heads, high[own], stats)
                stats = jnp.where(stat_lane == at_lane + 2 * heads, (total - high)[own], stats)
    both = jnp.concatenate(contexts + [stats.astype(bf16)], axis=1)
    out[...] = both.reshape(out.shape)


def merge_kernel(box, shelf_ids, live_mask, w_first, w_out, out, w_rest, arrived):
    rest_copy = pltpu.make_async_copy(w_out.at[:, w_first.shape[1] :], w_rest, arrived)
    rest_copy.start()
    chips, slots, wide = box.shape
    rows = chips * slots
    width = (wide - LANES) // CORES
    heads = width // DK
    requests = shelf_ids.shape[0]
    mine, live0, live1 = choose(shelf_ids[...], live_mask[...], chips, own_core())
    read = (live0 + live1) > 0.0
    got = box[...].reshape(rows, wide)
    stats = got[:, CORES * width :].astype(f32).T

    def stat(n):
        return jnp.concatenate([stats[n : n + 1], stats[3 * heads + n : 3 * heads + n + 1]], axis=1)

    shares = []
    totals = []
    for h in range(heads):
        peak = jnp.where(read, stat(h), far_below)
        best = jnp.max(peak, axis=1, keepdims=True)
        total = stat(heads + h) + stat(2 * heads + h)
        share = jnp.where(read, total * jnp.exp(peak - best), 0.0)
        shares.append(share)
        totals.append(jnp.sum(share, axis=1, keepdims=True))
    share = jnp.concatenate(shares, axis=0)
    high = share.astype(bf16)
    rest = (share - high.astype(f32)).astype(bf16)
    context = jnp.concatenate([got[:, :width], got[:, width : 2 * width]], axis=0)
    summed = dot(high, context, ((1,), (0,))) + dot(rest, context, ((1,), (0,)))
    head_of = lax.broadcasted_iota(jnp.int32, (requests, width), 1) // DK
    attended = jnp.zeros((requests, width), f32)
    for h in range(heads):
        part = summed[h * requests : (h + 1) * requests] / totals[h]
        attended = jnp.where(head_of == h, part, attended)
    attended = attended.astype(bf16)
    groups, _, columns = out.shape
    ahead = w_first.shape[1] // columns
    order = rotated(groups, groups // 2)
    for g in range(groups):
        if g == ahead:
            rest_copy.wait()
        at = g * columns if g < ahead else (g - ahead) * columns
        weights = (w_first if g < ahead else w_rest)[:, at : at + columns]
        out[order.index(g)] = dot(attended, weights, ((1,), (0,)))


def stage_kernel(*refs):
    count = (len(refs) - 1) // 2
    copies = [
        pltpu.make_async_copy(
            refs[n].at[tuple(pl.ds(0, k) for k in refs[count + n].shape)],
            refs[count + n],
            refs[-1].at[n],
        )
        for n in range(count)
    ]
    for copy in copies:
        copy.start()
    for copy in copies:
        copy.wait()


def in_vmem(shape, dtype):
    return pltpu.VMEM(shape, dtype)


def staged(shapes, arrays):
    return pl.pallas_call(
        stage_kernel,
        out_shape=[in_vmem(shape, a.dtype) for shape, a in zip(shapes, arrays)],
        in_specs=[pl.BlockSpec(memory_space=pl.ANY)] * len(arrays),
        out_specs=[pl.BlockSpec(memory_space=pltpu.VMEM)] * len(arrays),
        scratch_shapes=[pltpu.SemaphoreType.DMA((len(arrays),))],
        compiler_params=pltpu.CompilerParams(vmem_limit_bytes=1 << 20),
        name="stage",
    )(*[pltpu.with_memory_space_constraint(a, pltpu.HBM) for a in arrays])


def call(kernel, shape, dtype, name, near, far=(), hbm=(), scratch=()):
    spec = pl.BlockSpec(memory_space=pltpu.VMEM)
    near = [pltpu.with_memory_space_constraint(a, pltpu.VMEM) for a in near]
    far, hbm = [[pltpu.with_memory_space_constraint(a, pltpu.HBM) for a in some] for some in (far, hbm)]
    return pl.pallas_call(
        kernel,
        out_shape=in_vmem(shape, dtype),
        in_specs=[spec] * (len(near) + len(far)) + [pl.BlockSpec(memory_space=pl.ANY)] * len(hbm),
        out_specs=spec,
        scratch_shapes=list(scratch),
        compiler_params=pltpu.CompilerParams(vmem_limit_bytes=KERNEL_VMEM),
        name=name,
    )(*near, *far, *hbm)


def per_device(queries, passage_keys, passage_values, shelf_ids, live_mask, w_out):
    owners = lax.axis_size("psg")
    groups = lax.axis_size("head")
    requests, width = queries.shape

    def exchanged(x, axis, index_groups):
        return lax.all_to_all(
            x, axis, split_axis=0, concat_axis=0, axis_index_groups=index_groups, tiled=True
        )

    def from_other_core(x):
        return lax.ppermute(x, "psg", [(i, i ^ 1) for i in range(owners)])

    same_core = same_core_groups(owners)
    box_shape = (owners // CORES, SLOTS, CORES * width + LANES)
    box = call(box_kernel, box_shape, bf16, "box", (), (queries, shelf_ids, live_mask))
    ready = (passage_keys, passage_values, shelf_ids, live_mask, w_out)
    depth, columns = w_out.shape
    shapes = [a.shape for a in ready[:-1]] + [(depth, columns // 2)]
    keys, values, ids_near, live_near, w_first = staged(shapes, ready)
    partials = call(
        shelf_kernel,
        box_shape,
        bf16,
        "shelf",
        (
            exchanged(box, "psg", same_core),
            keys,
            values,
            from_other_core(passage_keys),
            from_other_core(passage_values),
        ),
    )
    projected = call(
        merge_kernel,
        (groups, requests, columns // groups),
        f32,
        "merge",
        (exchanged(partials, "psg", same_core), ids_near, live_near, w_first),
        hbm=(w_out,),
        scratch=(pltpu.VMEM((depth, columns - columns // 2), bf16), pltpu.SemaphoreType.DMA),
    )
    blocks = exchanged(projected, "head", [rotated(groups, groups // 2)])
    return jnp.sum(blocks, axis=0).astype(bf16)


def solution(mesh):
    in_specs = (
        P("psg", "head"),
        P("psg", None, "head"),
        P("psg", None, "head"),
        P("psg", None),
        P("psg", None),
        P("head", None),
    )
    out_specs = P("psg", "head")
    return jax.shard_map(
        per_device, mesh=mesh, in_specs=in_specs, out_specs=out_specs, check_vma=False
    )
```

time: 84.5 us -> 78.3 us (0.927)
  the two profiles are of different devices: /device:TPU:4 before, /device:TPU:2 now
where the time goes in v3:
time: 78.3 us; the launch traced here: 77.9 us
  blocking collectives  36.3 us (46%)
  starting transfers between devices  25.4 us (32%)
  waiting for transfers between devices  8.63 us (11%)
  Pallas kernels  6.91 us (9%)
    all_to_all x2, blocking collectives, exchanged(): lax.all_to_all(x, axis, split_axis=0, concat_axis=0, axis_index_groups=in...  36.3 us
    all_to_all x1, starting transfers between devices, exchanged(): lax.all_to_all(x, axis, split_axis=0, concat_axis=0, axis_index_groups=in...  21 us
    all_to_all x1, waiting for transfers between devices, exchanged(): lax.all_to_all(x, axis, split_axis=0, concat_axis=0, axis_index_groups=in...  8.55 us
    pallas_call x3, Pallas kernels, call(): pl.pallas_call(kernel, out_shape=in_vmem(shape, dtype), in_specs=[spec] *...  5.28 us
    ppermute x2, starting transfers between devices, from_other_core(): return lax.ppermute(x, 'psg', [(i, i ^ 1) for i in range(owners)])  4.33 us
    pallas_call x1, Pallas kernels, staged(): pl.pallas_call(stage_kernel, out_shape=[in_vmem(shape, a.dtype) for shape...  1.63 us
  transfers between devices with their start and end apart: 3, of which 2 were waited for; matrix products, arithmetic and copies ran while one was open for 0% of the time, Pallas kernels for 2%

profile of v3, /device:TPU:2, one launch (start us, length us, event | category | flops | bytes accessed | tf_op | source)
XLA Modules:
  0.0 77.9 jit_solution(18080987538813161359)
XLA Ops:
  0.0 1.8 %box.1 = bf16[64,2,1152]{2,1,0:T(2,128)(2,1)} custom-call(bf16[8,512]{1,0:T(8,128)(2,1)} %queries.1, s32[8,16]{1,0:T(8,128)} %refs_2_.1, s32[8,32]{1,0:T(8,128)} %refs_3_.1), custom_call_target="tpu_custom_call" | custom-call | tf_op jit(solution)/shard_map/box/pallas_call | solution.py:218
  1.8 21.0 %all-to-all-start = ((bf16[64,2,1152]{2,1,0:T(2,128)(2,1)}), bf16[64,2,1152]{2,1,0:T(2,128)(2,1)S(1)}, u32[]{:S(2)}, u32[]{:S(2)}) async-start(bf16[64,2,1152]{2,1,0:T(2,128)(2,1)} %box.1), calls=%async_computation | async-start | bytes 589824 | tf_op jit(solution)/shard_map/all_to_all | solution.py:235
  22.9 1.9 %collective-permute-start = (bf16[2,256,512]{2,1,0:T(8,128)(2,1)}, bf16[2,256,512]{2,1,0:T(8,128)(2,1)S(1)}, u32[]{:S(2)}, u32[]{:S(2)}) collective-permute-start(bf16[2,256,512]{2,1,0:T(8,128)(2,1)} %refs_0_.1), channel_id=1, source_target_pairs={{0,4},{4,0},{8,12},{12,8},{16,20},{20,16},{24,28},{28,24},{32,36},... | collective-permute-start | bytes 1572872 | tf_op jit(solution)/shard_map/ppermute | solution.py:240
  24.8 2.4 %collective-permute-start.1 = (bf16[2,256,512]{2,1,0:T(8,128)(2,1)}, bf16[2,256,512]{2,1,0:T(8,128)(2,1)S(1)}, u32[]{:S(2)}, u32[]{:S(2)}) collective-permute-start(bf16[2,256,512]{2,1,0:T(8,128)(2,1)} %refs_1_.1), channel_id=1, source_target_pairs={{0,4},{4,0},{8,12},{12,8},{16,20},{20,16},{24,28},{28,24},{32,36},... | collective-permute-start | bytes 1572872 | tf_op jit(solution)/shard_map/ppermute | solution.py:240
  27.2 1.6 %stage.1 = (bf16[2,256,512]{2,1,0:T(8,128)(2,1)S(1)}, bf16[2,256,512]{2,1,0:T(8,128)(2,1)S(1)}, s32[8,16]{1,0:T(8,128)S(1)}, s32[8,32]{1,0:T(8,128)S(1)}, bf16[512,1024]{1,0:T(8,128)(2,1)S(1)}) custom-call(bf16[2,256,512]{2,1,0:T(8,128)(2,1)} %refs_0_.1, bf16[2,256,512]{2,1,0:T(8,128)(2,1)} %refs_1_.1, s32[8,16]{1,0:T(8,128)} %refs_2_.1, s32[8,32]{1,0:T(8,128)} %refs_3_.1, ...), custom_call_target="tpu_custom_call" | custom-call | tf_op jit(solution)/shard_map/stage/pallas_call | solution.py:203
  28.9 0.0 collective-permute-done.other_keys
  28.9 0.1 collective-permute-done.1.other_values
  29.0 8.6 %all-to-all-done.box = bf16[64,2,1152]{2,1,0:T(2,128)(2,1)S(1)} async-done(((bf16[64,2,1152]{2,1,0:T(2,128)(2,1)}), bf16[64,2,1152]{2,1,0:T(2,128)(2,1)S(1)}, u32[]{:S(2)}, u32[]{:S(2)}) %all-to-all-start) | async-done | bytes 294944 | tf_op jit(solution)/shard_map/all_to_all | solution.py:235
  37.5 1.9 %shelf.1 = bf16[64,2,1152]{2,1,0:T(2,128)(2,1)S(1)} custom-call(bf16[64,2,1152]{2,1,0:T(2,128)(2,1)S(1)} %all-to-all-done.box, bf16[2,256,512]{2,1,0:T(8,128)(2,1)S(1)} %get-tuple-element.10.keys, bf16[2,256,512]{2,1,0:T(8,128)(2,1)S(1)} %get-tuple-element.11.values, bf16[2,256,512]{2,1,0:T(8,128)(2,1)S(1)} %collective-permute-done.other_keys, ...), custom_call_target="tpu_custom_call" | custom-call | tf_op jit(solution)/shard_map/shelf/pallas_call | solution.py:218
  39.5 28.3 %all_to_all.15.box = bf16[64,2,1152]{2,1,0:T(2,128)(2,1)S(1)} all-to-all(bf16[64,2,1152]{2,1,0:T(2,128)(2,1)S(1)} %shelf.1), channel_id=1, replica_groups={{272,280,288,296,304,312,320,328,336,344,352,360,368,376,384,392,400,40..., dimensions={0} | all-to-all | bytes 589824 | tf_op jit(solution)/shard_map/all_to_all | solution.py:235
  67.7 1.5 %merge.1 = f32[4,8,512]{2,1,0:T(8,128)S(1)} custom-call(bf16[64,2,1152]{2,1,0:T(2,128)(2,1)S(1)} %all_to_all.15.box, s32[8,16]{1,0:T(8,128)S(1)} %get-tuple-element.12.shelf_ids, s32[8,32]{1,0:T(8,128)S(1)} %get-tuple-element.13.live_mask, bf16[512,1024]{1,0:T(8,128)(2,1)S(1)} %get-tuple-element.14.w_first, bf16[512,2048]{1,0:T(8,128)(2,1)} %w_out.1), custom_call_target="tpu_custom_call" | custom-call | tf_op jit(solution)/shard_map/merge/pallas_call | solution.py:218
  69.3 8.0 %all_to_all.16 = f32[4,8,512]{2,1,0:T(8,128)S(1)} all-to-all(f32[4,8,512]{2,1,0:T(8,128)S(1)} %merge.1), channel_id=1, replica_groups={{2,3,0,1},{6,7,4,5},{10,11,8,9},{14,15,12,13},{18,19,16,17},{22,23,20,2..., dimensions={0} | all-to-all | bytes 131072 | tf_op jit(solution)/shard_map/all_to_all | solution.py:235
  77.3 0.6 reduce_sum.9
Async XLA Ops:
  1.8 35.7 %all-to-all-start = ((bf16[64,2,1152]{2,1,0:T(2,128)(2,1)}), bf16[64,2,1152]{2,1,0:T(2,128)(2,1)S(1)}, u32[]{:S(2)}, u32[]{:S(2)}) async-start(bf16[64,2,1152]{2,1,0:T(2,128)(2,1)} %box.1), calls=%async_computation | async-start | bytes 589824 | tf_op jit(solution)/shard_map/all_to_all | solution.py:235
  22.9 6.0 %collective-permute-start = (bf16[2,256,512]{2,1,0:T(8,128)(2,1)}, bf16[2,256,512]{2,1,0:T(8,128)(2,1)S(1)}, u32[]{:S(2)}, u32[]{:S(2)}) collective-permute-start(bf16[2,256,512]{2,1,0:T(8,128)(2,1)} %refs_0_.1), channel_id=1, source_target_pairs={{0,4},{4,0},{8,12},{12,8},{16,20},{20,16},{24,28},{28,24},{32,36},... | collective-permute-start | bytes 1572872 | tf_op jit(solution)/shard_map/ppermute | solution.py:240
  24.8 4.1 %collective-permute-start.1 = (bf16[2,256,512]{2,1,0:T(8,128)(2,1)}, bf16[2,256,512]{2,1,0:T(8,128)(2,1)S(1)}, u32[]{:S(2)}, u32[]{:S(2)}) collective-permute-start(bf16[2,256,512]{2,1,0:T(8,128)(2,1)} %refs_1_.1), channel_id=1, source_target_pairs={{0,4},{4,0},{8,12},{12,8},{16,20},{20,16},{24,28},{28,24},{32,36},... | collective-permute-start | bytes 1572872 | tf_op jit(solution)/shard_map/ppermute | solution.py:240

commit v4 on v3

--- a/solution.py
+++ b/solution.py
@@ -16,7 +16,7 @@
 
 
 def first_chip(chips):
-    return chips // 2 + chips // 32 if chips >= 32 else 0
+    return chips * 45 // 64 if chips >= 32 else 0
 
 
 def rotated(length, first):
@@ -86,14 +86,16 @@
     box[...] = both.reshape(box.shape)
 
 
-def shelf_kernel(box, keys, values, other_keys, other_values, out):
+def shelf_kernel(box, keys, values, other_keys, other_values, w_out, out, w_near, got, arrived):
+    w_copy = pltpu.make_async_copy(w_out, w_near, arrived)
+    w_copy.start()
     chips, slots, wide = box.shape
     rows = chips * slots
     width = (wide - LANES) // CORES
     passages, length, _ = keys.shape
     positions = passages * length
     heads = width // DK
-    got = box[...].reshape(rows, wide)
+    got[...] = box[...].reshape(rows, wide)
     flags = got[:, CORES * width :]
     flags = jnp.concatenate([flags, flags], axis=0)
     place = lax.broadcasted_iota(jnp.int32, (positions, LANES), 0) // length
@@ -130,11 +132,10 @@
                 stats = jnp.where(stat_lane == at_lane + 2 * heads, (total - high)[own], stats)
     both = jnp.concatenate(contexts + [stats.astype(bf16)], axis=1)
     out[...] = both.reshape(out.shape)
-
-
-def merge_kernel(box, shelf_ids, live_mask, w_first, w_out, out, w_rest, arrived):
-    rest_copy = pltpu.make_async_copy(w_out.at[:, w_first.shape[1] :], w_rest, arrived)
-    rest_copy.start()
+    w_copy.wait()
+
+
+def merge_kernel(box, w_out, shelf_ids, live_mask, out, got):
     chips, slots, wide = box.shape
     rows = chips * slots
     width = (wide - LANES) // CORES
@@ -142,7 +143,7 @@
     requests = shelf_ids.shape[0]
     mine, live0, live1 = choose(shelf_ids[...], live_mask[...], chips, own_core())
     read = (live0 + live1) > 0.0
-    got = box[...].reshape(rows, wide)
+    got[...] = box[...].reshape(rows, wide)
     stats = got[:, CORES * width :].astype(f32).T
 
     def stat(n):
@@ -169,14 +170,8 @@
         attended = jnp.where(head_of == h, part, attended)
     attended = attended.astype(bf16)
     groups, _, columns = out.shape
-    ahead = w_first.shape[1] // columns
-    order = rotated(groups, groups // 2)
-    for g in range(groups):
-        if g == ahead:
-            rest_copy.wait()
-        at = g * columns if g < ahead else (g - ahead) * columns
-        weights = (w_first if g < ahead else w_rest)[:, at : at + columns]
-        out[order.index(g)] = dot(attended, weights, ((1,), (0,)))
+    for n, g in enumerate(rotated(groups, groups // 2)):
+        out[n] = dot(attended, w_out[:, g * columns : (g + 1) * columns], ((1,), (0,)))
 
 
 def stage_kernel(*refs):
@@ -199,10 +194,10 @@
     return pltpu.VMEM(shape, dtype)
 
 
-def staged(shapes, arrays):
+def staged(*arrays):
     return pl.pallas_call(
         stage_kernel,
-        out_shape=[in_vmem(shape, a.dtype) for shape, a in zip(shapes, arrays)],
+        out_shape=[in_vmem(a.shape, a.dtype) for a in arrays],
         in_specs=[pl.BlockSpec(memory_space=pl.ANY)] * len(arrays),
         out_specs=[pl.BlockSpec(memory_space=pltpu.VMEM)] * len(arrays),
         scratch_shapes=[pltpu.SemaphoreType.DMA((len(arrays),))],
@@ -211,15 +206,17 @@
     )(*[pltpu.with_memory_space_constraint(a, pltpu.HBM) for a in arrays])
 
 
-def call(kernel, shape, dtype, name, near, far=(), hbm=(), scratch=()):
+def call(kernel, results, name, near, far=(), hbm=(), scratch=()):
     spec = pl.BlockSpec(memory_space=pltpu.VMEM)
     near = [pltpu.with_memory_space_constraint(a, pltpu.VMEM) for a in near]
-    far, hbm = [[pltpu.with_memory_space_constraint(a, pltpu.HBM) for a in some] for some in (far, hbm)]
+    far, hbm = [
+        [pltpu.with_memory_space_constraint(a, pltpu.HBM) for a in some] for some in (far, hbm)
+    ]
     return pl.pallas_call(
         kernel,
-        out_shape=in_vmem(shape, dtype),
+        out_shape=[in_vmem(*result) for result in results],
         in_specs=[spec] * (len(near) + len(far)) + [pl.BlockSpec(memory_space=pl.ANY)] * len(hbm),
-        out_specs=spec,
+        out_specs=[spec] * len(results),
         scratch_shapes=list(scratch),
         compiler_params=pltpu.CompilerParams(vmem_limit_bytes=KERNEL_VMEM),
         name=name,
@@ -240,16 +237,15 @@
         return lax.ppermute(x, "psg", [(i, i ^ 1) for i in range(owners)])
 
     same_core = same_core_groups(owners)
-    box_shape = (owners // CORES, SLOTS, CORES * width + LANES)
-    box = call(box_kernel, box_shape, bf16, "box", (), (queries, shelf_ids, live_mask))
-    ready = (passage_keys, passage_values, shelf_ids, live_mask, w_out)
-    depth, columns = w_out.shape
-    shapes = [a.shape for a in ready[:-1]] + [(depth, columns // 2)]
-    keys, values, ids_near, live_near, w_first = staged(shapes, ready)
-    partials = call(
+    chips = owners // CORES
+    wide = CORES * width + LANES
+    box_array = ((chips, SLOTS, wide), bf16)
+    rows = pltpu.VMEM((chips * SLOTS, wide), bf16)
+    (box,) = call(box_kernel, [box_array], "box", (), (queries, shelf_ids, live_mask))
+    keys, values, ids_near, live_near = staged(passage_keys, passage_values, shelf_ids, live_mask)
+    partials, w_near = call(
         shelf_kernel,
-        box_shape,
-        bf16,
+        [box_array, (w_out.shape, w_out.dtype)],
         "shelf",
         (
             exchanged(box, "psg", same_core),
@@ -258,15 +254,15 @@
             from_other_core(passage_keys),
             from_other_core(passage_values),
         ),
-    )
-    projected = call(
+        hbm=(w_out,),
+        scratch=(rows, pltpu.SemaphoreType.DMA),
+    )
+    (projected,) = call(
         merge_kernel,
-        (groups, requests, columns // groups),
-        f32,
+        [((groups, requests, w_out.shape[1] // groups), f32)],
         "merge",
-        (exchanged(partials, "psg", same_core), ids_near, live_near, w_first),
-        hbm=(w_out,),
-        scratch=(pltpu.VMEM((depth, columns - columns // 2), bf16), pltpu.SemaphoreType.DMA),
+        (exchanged(partials, "psg", same_core), w_near, ids_near, live_near),
+        scratch=(rows,),
     )
     blocks = exchanged(projected, "head", [rotated(groups, groups // 2)])
     return jnp.sum(blocks, axis=0).astype(bf16)

time: 78.3 us -> 76.3 us (0.974)
  the two profiles are of different devices: /device:TPU:2 before, /device:TPU:16 now
where the time goes in v4:
time: 76.3 us; the launch traced here: 76 us
  blocking collectives  36.1 us (47%)
  starting transfers between devices  23.5 us (31%)
  waiting for transfers between devices  10.2 us (13%)
  Pallas kernels  5.59 us (7%)
    all_to_all x2, blocking collectives, exchanged(): lax.all_to_all(x, axis, split_axis=0, concat_axis=0, axis_index_groups=in...  36.1 us
    all_to_all x1, starting transfers between devices, exchanged(): lax.all_to_all(x, axis, split_axis=0, concat_axis=0, axis_index_groups=in...  19.2 us
    all_to_all x1, waiting for transfers between devices, exchanged(): lax.all_to_all(x, axis, split_axis=0, concat_axis=0, axis_index_groups=in...  9.69 us
    pallas_call x3, Pallas kernels, call(): pl.pallas_call(kernel, out_shape=[in_vmem(*result) for result in results]...  4.35 us
    ppermute x2, starting transfers between devices, from_other_core(): return lax.ppermute(x, 'psg', [(i, i ^ 1) for i in range(owners)])  4.33 us
  transfers between devices with their start and end apart: 3, of which 2 were waited for; matrix products, arithmetic and copies ran while one was open for 0% of the time, Pallas kernels for 2%

profile of v4, /device:TPU:16, one launch (start us, length us, event | category | flops | bytes accessed | tf_op | source)
XLA Modules:
  0.0 76.0 jit_solution(8006679090758609781)
XLA Ops:
  0.0 1.9 %box.1 = bf16[64,2,1152]{2,1,0:T(2,128)(2,1)} custom-call(bf16[8,512]{1,0:T(8,128)(2,1)} %queries.1, s32[8,16]{1,0:T(8,128)} %refs_2_.1, s32[8,32]{1,0:T(8,128)} %refs_3_.1), custom_call_target="tpu_custom_call" | custom-call | tf_op jit(solution)/shard_map/box/pallas_call | solution.py:215
  1.9 19.2 %all-to-all-start = ((bf16[64,2,1152]{2,1,0:T(2,128)(2,1)}), bf16[64,2,1152]{2,1,0:T(2,128)(2,1)S(1)}, u32[]{:S(2)}, u32[]{:S(2)}) async-start(bf16[64,2,1152]{2,1,0:T(2,128)(2,1)} %box.1), calls=%async_computation | async-start | bytes 589824 | tf_op jit(solution)/shard_map/all_to_all | solution.py:232
  21.1 1.9 %collective-permute-start = (bf16[2,256,512]{2,1,0:T(8,128)(2,1)}, bf16[2,256,512]{2,1,0:T(8,128)(2,1)S(1)}, u32[]{:S(2)}, u32[]{:S(2)}) collective-permute-start(bf16[2,256,512]{2,1,0:T(8,128)(2,1)} %refs_0_.1), channel_id=1, source_target_pairs={{0,4},{4,0},{8,12},{12,8},{16,20},{20,16},{24,28},{28,24},{32,36},... | collective-permute-start | bytes 1572872 | tf_op jit(solution)/shard_map/ppermute | solution.py:237
  23.0 2.4 %collective-permute-start.1 = (bf16[2,256,512]{2,1,0:T(8,128)(2,1)}, bf16[2,256,512]{2,1,0:T(8,128)(2,1)S(1)}, u32[]{:S(2)}, u32[]{:S(2)}) collective-permute-start(bf16[2,256,512]{2,1,0:T(8,128)(2,1)} %refs_1_.1), channel_id=1, source_target_pairs={{0,4},{4,0},{8,12},{12,8},{16,20},{20,16},{24,28},{28,24},{32,36},... | collective-permute-start | bytes 1572872 | tf_op jit(solution)/shard_map/ppermute | solution.py:237
  25.4 1.2 %stage.1 = (bf16[2,256,512]{2,1,0:T(8,128)(2,1)S(1)}, bf16[2,256,512]{2,1,0:T(8,128)(2,1)S(1)}, s32[8,16]{1,0:T(8,128)S(1)}, s32[8,32]{1,0:T(8,128)S(1)}) custom-call(bf16[2,256,512]{2,1,0:T(8,128)(2,1)} %refs_0_.1, bf16[2,256,512]{2,1,0:T(8,128)(2,1)} %refs_1_.1, s32[8,16]{1,0:T(8,128)} %refs_2_.1, s32[8,32]{1,0:T(8,128)} %refs_3_.1), custom_call_target="tpu_custom_call" | custom-call | tf_op jit(solution)/shard_map/stage/pallas_call | solution.py:198
  26.7 0.0 collective-permute-done.other_keys
  26.7 0.5 collective-permute-done.1.other_values
  27.1 9.7 %all-to-all-done.box = bf16[64,2,1152]{2,1,0:T(2,128)(2,1)S(1)} async-done(((bf16[64,2,1152]{2,1,0:T(2,128)(2,1)}), bf16[64,2,1152]{2,1,0:T(2,128)(2,1)S(1)}, u32[]{:S(2)}, u32[]{:S(2)}) %all-to-all-start) | async-done | bytes 294944 | tf_op jit(solution)/shard_map/all_to_all | solution.py:232
  36.8 1.7 %shelf.1 = (bf16[64,2,1152]{2,1,0:T(2,128)(2,1)S(1)}, bf16[512,2048]{1,0:T(8,128)(2,1)S(1)}) custom-call(bf16[64,2,1152]{2,1,0:T(2,128)(2,1)S(1)} %all-to-all-done.box, bf16[2,256,512]{2,1,0:T(8,128)(2,1)S(1)} %get-tuple-element.11.keys, bf16[2,256,512]{2,1,0:T(8,128)(2,1)S(1)} %get-tuple-element.12.values, ...), custom_call_target="tpu_custom_call" | custom-call | tf_op jit(solution)/shard_map/shelf/pallas_call | solution.py:215
  38.5 28.1 %all_to_all.15.box = bf16[64,2,1152]{2,1,0:T(2,128)(2,1)S(1)} all-to-all(bf16[64,2,1152]{2,1,0:T(2,128)(2,1)S(1)} %get-tuple-element.13), channel_id=1, replica_groups={{360,368,376,384,392,400,408,416,424,432,440,448,456,464,472,480,488,49..., dimensions={0} | all-to-all | bytes 589824 | tf_op jit(solution)/shard_map/all_to_all | solution.py:232
  66.6 0.8 %merge.1 = f32[4,8,512]{2,1,0:T(8,128)S(1)} custom-call(bf16[64,2,1152]{2,1,0:T(2,128)(2,1)S(1)} %all_to_all.15.box, bf16[512,2048]{1,0:T(8,128)(2,1)S(1)} %get-tuple-element.14.w_out, s32[8,16]{1,0:T(8,128)S(1)} %get-tuple-element.15.shelf_ids, s32[8,32]{1,0:T(8,128)S(1)} %get-tuple-element.16.live_mask), custom_call_target="tpu_custom_call" | custom-call | tf_op jit(solution)/shard_map/merge/pallas_call | solution.py:215
  67.4 8.0 %all_to_all.16 = f32[4,8,512]{2,1,0:T(8,128)S(1)} all-to-all(f32[4,8,512]{2,1,0:T(8,128)S(1)} %merge.1), channel_id=1, replica_groups={{2,3,0,1},{6,7,4,5},{10,11,8,9},{14,15,12,13},{18,19,16,17},{22,23,20,2..., dimensions={0} | all-to-all | bytes 131072 | tf_op jit(solution)/shard_map/all_to_all | solution.py:232
  75.4 0.6 reduce_sum.9
Async XLA Ops:
  1.9 35.0 %all-to-all-start = ((bf16[64,2,1152]{2,1,0:T(2,128)(2,1)}), bf16[64,2,1152]{2,1,0:T(2,128)(2,1)S(1)}, u32[]{:S(2)}, u32[]{:S(2)}) async-start(bf16[64,2,1152]{2,1,0:T(2,128)(2,1)} %box.1), calls=%async_computation | async-start | bytes 589824 | tf_op jit(solution)/shard_map/all_to_all | solution.py:232
  21.1 5.6 %collective-permute-start = (bf16[2,256,512]{2,1,0:T(8,128)(2,1)}, bf16[2,256,512]{2,1,0:T(8,128)(2,1)S(1)}, u32[]{:S(2)}, u32[]{:S(2)}) collective-permute-start(bf16[2,256,512]{2,1,0:T(8,128)(2,1)} %refs_0_.1), channel_id=1, source_target_pairs={{0,4},{4,0},{8,12},{12,8},{16,20},{20,16},{24,28},{28,24},{32,36},... | collective-permute-start | bytes 1572872 | tf_op jit(solution)/shard_map/ppermute | solution.py:237
  23.0 4.1 %collective-permute-start.1 = (bf16[2,256,512]{2,1,0:T(8,128)(2,1)}, bf16[2,256,512]{2,1,0:T(8,128)(2,1)S(1)}, u32[]{:S(2)}, u32[]{:S(2)}) collective-permute-start(bf16[2,256,512]{2,1,0:T(8,128)(2,1)} %refs_1_.1), channel_id=1, source_target_pairs={{0,4},{4,0},{8,12},{12,8},{16,20},{20,16},{24,28},{28,24},{32,36},... | collective-permute-start | bytes 1572872 | tf_op jit(solution)/shard_map/ppermute | solution.py:237

commit v5 on v4

--- a/solution.py
+++ b/solution.py
@@ -104,7 +104,8 @@
     stat_lane = lax.broadcasted_iota(jnp.int32, (rows, LANES), 1)
     low = stat_lane < DK
     keep = [jnp.where(low, 1.0, 0.0).astype(bf16), jnp.where(low, 0.0, 1.0).astype(bf16)]
-    stats = jnp.zeros((rows, LANES), f32)
+    peaks = jnp.zeros((rows, LANES), f32)
+    totals = jnp.zeros((rows, LANES), f32)
     contexts = []
     for shelf, (key_ref, value_ref) in enumerate(((keys, values), (other_keys, other_values))):
         bias = jnp.where(place + passages * shelf == lane, far_below, 0.0).astype(bf16)
@@ -123,38 +124,41 @@
             total = summed[:, LANES:]
             context = summed[:, :LANES] / total
             contexts.append(jnp.where(low, context[:rows], context[rows:]).astype(bf16))
-            high = total.astype(bf16).astype(f32)
             for part in range(2):
                 own = slice(part * rows, (part + 1) * rows)
-                at_lane = 3 * heads * shelf + 2 * pair + part
-                stats = jnp.where(stat_lane == at_lane, peak[own], stats)
-                stats = jnp.where(stat_lane == at_lane + heads, high[own], stats)
-                stats = jnp.where(stat_lane == at_lane + 2 * heads, (total - high)[own], stats)
+                here = stat_lane == heads * shelf + 2 * pair + part
+                peaks = jnp.where(here, peak[own], peaks)
+                totals = jnp.where(here, total[own], totals)
+    count = CORES * heads
+    high = totals.astype(bf16).astype(f32)
+    low_part = pltpu.roll(totals - high, 2 * count, 1)
+    stats = jnp.where(stat_lane < 2 * count, pltpu.roll(high, count, 1), low_part)
+    stats = jnp.where(stat_lane < count, peaks, stats)
     both = jnp.concatenate(contexts + [stats.astype(bf16)], axis=1)
     out[...] = both.reshape(out.shape)
     w_copy.wait()
 
 
-def merge_kernel(box, w_out, shelf_ids, live_mask, out, got):
+def merge_kernel(box, w_out, reads, out, got):
     chips, slots, wide = box.shape
     rows = chips * slots
     width = (wide - LANES) // CORES
     heads = width // DK
-    requests = shelf_ids.shape[0]
-    mine, live0, live1 = choose(shelf_ids[...], live_mask[...], chips, own_core())
-    read = (live0 + live1) > 0.0
+    requests = reads.shape[0]
+    read = reads[...] > 0.0
     got[...] = box[...].reshape(rows, wide)
     stats = got[:, CORES * width :].astype(f32).T
 
-    def stat(n):
-        return jnp.concatenate([stats[n : n + 1], stats[3 * heads + n : 3 * heads + n + 1]], axis=1)
+    def stat(kind, h):
+        at = kind * CORES * heads + h
+        return jnp.concatenate([stats[at : at + 1], stats[at + heads : at + heads + 1]], axis=1)
 
     shares = []
     totals = []
     for h in range(heads):
-        peak = jnp.where(read, stat(h), far_below)
+        peak = jnp.where(read, stat(0, h), far_below)
         best = jnp.max(peak, axis=1, keepdims=True)
-        total = stat(heads + h) + stat(2 * heads + h)
+        total = stat(1, h) + stat(2, h)
         share = jnp.where(read, total * jnp.exp(peak - best), 0.0)
         shares.append(share)
         totals.append(jnp.sum(share, axis=1, keepdims=True))
@@ -174,18 +178,16 @@
         out[n] = dot(attended, w_out[:, g * columns : (g + 1) * columns], ((1,), (0,)))
 
 
-def stage_kernel(*refs):
-    count = (len(refs) - 1) // 2
+def stage_kernel(shelf_ids, live_mask, keys, values, near_keys, near_values, reads, arrived):
     copies = [
-        pltpu.make_async_copy(
-            refs[n].at[tuple(pl.ds(0, k) for k in refs[count + n].shape)],
-            refs[count + n],
-            refs[-1].at[n],
-        )
-        for n in range(count)
+        pltpu.make_async_copy(keys, near_keys, arrived.at[0]),
+        pltpu.make_async_copy(values, near_values, arrived.at[1]),
     ]
     for copy in copies:
         copy.start()
+    chips = reads.shape[1] // (CORES * SLOTS)
+    _, live0, live1 = choose(shelf_ids[...], live_mask[...], chips, own_core())
+    reads[...] = live0 + live1
     for copy in copies:
         copy.wait()
 
@@ -194,19 +196,7 @@
     return pltpu.VMEM(shape, dtype)
 
 
-def staged(*arrays):
-    return pl.pallas_call(
-        stage_kernel,
-        out_shape=[in_vmem(a.shape, a.dtype) for a in arrays],
-        in_specs=[pl.BlockSpec(memory_space=pl.ANY)] * len(arrays),
-        out_specs=[pl.BlockSpec(memory_space=pltpu.VMEM)] * len(arrays),
-        scratch_shapes=[pltpu.SemaphoreType.DMA((len(arrays),))],
-        compiler_params=pltpu.CompilerParams(vmem_limit_bytes=1 << 20),
-        name="stage",
-    )(*[pltpu.with_memory_space_constraint(a, pltpu.HBM) for a in arrays])
-
-
-def call(kernel, results, name, near, far=(), hbm=(), scratch=()):
+def call(kernel, results, name, near, far=(), hbm=(), scratch=(), room=KERNEL_VMEM):
     spec = pl.BlockSpec(memory_space=pltpu.VMEM)
     near = [pltpu.with_memory_space_constraint(a, pltpu.VMEM) for a in near]
     far, hbm = [
@@ -218,7 +208,7 @@
         in_specs=[spec] * (len(near) + len(far)) + [pl.BlockSpec(memory_space=pl.ANY)] * len(hbm),
         out_specs=[spec] * len(results),
         scratch_shapes=list(scratch),
-        compiler_params=pltpu.CompilerParams(vmem_limit_bytes=KERNEL_VMEM),
+        compiler_params=pltpu.CompilerParams(vmem_limit_bytes=room),
         name=name,
     )(*near, *far, *hbm)
 
@@ -242,7 +232,20 @@
     box_array = ((chips, SLOTS, wide), bf16)
     rows = pltpu.VMEM((chips * SLOTS, wide), bf16)
     (box,) = call(box_kernel, [box_array], "box", (), (queries, shelf_ids, live_mask))
-    keys, values, ids_near, live_near = staged(passage_keys, passage_values, shelf_ids, live_mask)
+    keys, values, reads = call(
+        stage_kernel,
+        [
+            (passage_keys.shape, bf16),
+            (passage_values.shape, bf16),
+            ((requests, CORES * SLOTS * chips), f32),
+        ],
+        "stage",
+        (),
+        (shelf_ids, live_mask),
+        (passage_keys, passage_values),
+        (pltpu.SemaphoreType.DMA((2,)),),
+        2 << 20,
+    )
     partials, w_near = call(
         shelf_kernel,
         [box_array, (w_out.shape, w_out.dtype)],
@@ -261,7 +264,7 @@
         merge_kernel,
         [((groups, requests, w_out.shape[1] // groups), f32)],
         "merge",
-        (exchanged(partials, "psg", same_core), w_near, ids_near, live_near),
+        (exchanged(partials, "psg", same_core), w_near, reads),
         scratch=(rows,),
     )
     blocks = exchanged(projected, "head", [rotated(groups, groups // 2)])

time: 76.3 us -> 76.4 us (level)
    pallas_call x3 -> x4, Pallas kernels: 4.35 us -> 6.24 us  [call(): pl.pallas_call(kernel, out_shape=[in_vmem(*result) for result in results]...]
    pallas_call x1 -> x0, Pallas kernels: 1.24 us -> none  [staged(): pl.pallas_call(stage_kernel, out_shape=[in_vmem(a.shape, a.dtype) for a i...]
  transfers between devices with their start and end apart: 3 -> 3, of which waited for: 2 -> 1; matrix products, arithmetic and copies ran while one was open for 0% -> 0% of each run, Pallas kernels for 2% -> 3%
where the time goes in v5:
time: 76.4 us; the launch traced here: 76 us
  blocking collectives  36.1 us (47%)
  starting transfers between devices  23.5 us (31%)
  waiting for transfers between devices  9.47 us (12%)
  Pallas kernels  6.24 us (8%)
    all_to_all x2, blocking collectives, exchanged(): lax.all_to_all(x, axis, split_axis=0, concat_axis=0, axis_index_groups=in...  36.1 us
    all_to_all x1, starting transfers between devices, exchanged(): lax.all_to_all(x, axis, split_axis=0, concat_axis=0, axis_index_groups=in...  19.2 us
    all_to_all x1, waiting for transfers between devices, exchanged(): lax.all_to_all(x, axis, split_axis=0, concat_axis=0, axis_index_groups=in...  9.47 us
    pallas_call x4, Pallas kernels, call(): pl.pallas_call(kernel, out_shape=[in_vmem(*result) for result in results]...  6.24 us
    ppermute x2, starting transfers between devices, from_other_core(): return lax.ppermute(x, 'psg', [(i, i ^ 1) for i in range(owners)])  4.33 us
  transfers between devices with their start and end apart: 3, of which 1 were waited for; matrix products, arithmetic and copies ran while one was open for 0% of the time, Pallas kernels for 3%

profile of v5, /device:TPU:16, one launch (start us, length us, event | category | flops | bytes accessed | tf_op | source)
XLA Modules:
  0.0 76.0 jit_solution(6256737096297654585)
XLA Ops:
  0.0 1.9 %box.1 = bf16[64,2,1152]{2,1,0:T(2,128)(2,1)} custom-call(bf16[8,512]{1,0:T(8,128)(2,1)} %queries.1, s32[8,16]{1,0:T(8,128)} %shelf_ids.3, s32[8,32]{1,0:T(8,128)} %live_mask.3), custom_call_target="tpu_custom_call" | custom-call | tf_op jit(solution)/shard_map/box/pallas_call | solution.py:205
  1.9 19.2 %all-to-all-start = ((bf16[64,2,1152]{2,1,0:T(2,128)(2,1)}), bf16[64,2,1152]{2,1,0:T(2,128)(2,1)S(1)}, u32[]{:S(2)}, u32[]{:S(2)}) async-start(bf16[64,2,1152]{2,1,0:T(2,128)(2,1)} %box.1), calls=%async_computation | async-start | bytes 589824 | tf_op jit(solution)/shard_map/all_to_all | solution.py:222
  21.1 1.9 %collective-permute-start = (bf16[2,256,512]{2,1,0:T(8,128)(2,1)}, bf16[2,256,512]{2,1,0:T(8,128)(2,1)S(1)}, u32[]{:S(2)}, u32[]{:S(2)}) collective-permute-start(bf16[2,256,512]{2,1,0:T(8,128)(2,1)} %keys.1), channel_id=1, source_target_pairs={{0,4},{4,0},{8,12},{12,8},{16,20},{20,16},{24,28},{28,24},{32,36},... | collective-permute-start | bytes 1572872 | tf_op jit(solution)/shard_map/ppermute | solution.py:227
  23.0 2.4 %collective-permute-start.1 = (bf16[2,256,512]{2,1,0:T(8,128)(2,1)}, bf16[2,256,512]{2,1,0:T(8,128)(2,1)S(1)}, u32[]{:S(2)}, u32[]{:S(2)}) collective-permute-start(bf16[2,256,512]{2,1,0:T(8,128)(2,1)} %values.1), channel_id=1, source_target_pairs={{0,4},{4,0},{8,12},{12,8},{16,20},{20,16},{24,28},{28,24},{32,36},... | collective-permute-start | bytes 1572872 | tf_op jit(solution)/shard_map/ppermute | solution.py:227
  25.4 1.9 %stage.1 = (bf16[2,256,512]{2,1,0:T(8,128)(2,1)S(1)}, bf16[2,256,512]{2,1,0:T(8,128)(2,1)S(1)}, f32[8,256]{1,0:T(8,128)S(1)}) custom-call(s32[8,16]{1,0:T(8,128)} %shelf_ids.3, s32[8,32]{1,0:T(8,128)} %live_mask.3, bf16[2,256,512]{2,1,0:T(8,128)(2,1)} %keys.1, bf16[2,256,512]{2,1,0:T(8,128)(2,1)} %values.1), custom_call_target="tpu_custom_call" | custom-call | tf_op jit(solution)/shard_map/stage/pallas_call | solution.py:205
  27.3 0.0 collective-permute-done.other_keys
  27.3 0.0 collective-permute-done.1.other_values
  27.4 9.5 %all-to-all-done.box = bf16[64,2,1152]{2,1,0:T(2,128)(2,1)S(1)} async-done(((bf16[64,2,1152]{2,1,0:T(2,128)(2,1)}), bf16[64,2,1152]{2,1,0:T(2,128)(2,1)S(1)}, u32[]{:S(2)}, u32[]{:S(2)}) %all-to-all-start) | async-done | bytes 294944 | tf_op jit(solution)/shard_map/all_to_all | solution.py:222
  36.8 1.8 %shelf.1 = (bf16[64,2,1152]{2,1,0:T(2,128)(2,1)S(1)}, bf16[512,2048]{1,0:T(8,128)(2,1)S(1)}) custom-call(bf16[64,2,1152]{2,1,0:T(2,128)(2,1)S(1)} %all-to-all-done.box, bf16[2,256,512]{2,1,0:T(8,128)(2,1)S(1)} %get-tuple-element.10.keys, bf16[2,256,512]{2,1,0:T(8,128)(2,1)S(1)} %get-tuple-element.11.values, ...), custom_call_target="tpu_custom_call" | custom-call | tf_op jit(solution)/shard_map/shelf/pallas_call | solution.py:205
  38.6 28.1 %all_to_all.15.box = bf16[64,2,1152]{2,1,0:T(2,128)(2,1)S(1)} all-to-all(bf16[64,2,1152]{2,1,0:T(2,128)(2,1)S(1)} %get-tuple-element.12), channel_id=1, replica_groups={{360,368,376,384,392,400,408,416,424,432,440,448,456,464,472,480,488,49..., dimensions={0} | all-to-all | bytes 589824 | tf_op jit(solution)/shard_map/all_to_all | solution.py:222
  66.6 0.7 merge.1
  67.4 8.0 %all_to_all.16 = f32[4,8,512]{2,1,0:T(8,128)S(1)} all-to-all(f32[4,8,512]{2,1,0:T(8,128)S(1)} %merge.1), channel_id=1, replica_groups={{2,3,0,1},{6,7,4,5},{10,11,8,9},{14,15,12,13},{18,19,16,17},{22,23,20,2..., dimensions={0} | all-to-all | bytes 131072 | tf_op jit(solution)/shard_map/all_to_all | solution.py:222
  75.3 0.6 reduce_sum.9
Async XLA Ops:
  1.9 35.0 %all-to-all-start = ((bf16[64,2,1152]{2,1,0:T(2,128)(2,1)}), bf16[64,2,1152]{2,1,0:T(2,128)(2,1)S(1)}, u32[]{:S(2)}, u32[]{:S(2)}) async-start(bf16[64,2,1152]{2,1,0:T(2,128)(2,1)} %box.1), calls=%async_computation | async-start | bytes 589824 | tf_op jit(solution)/shard_map/all_to_all | solution.py:222
  21.1 6.3 %collective-permute-start = (bf16[2,256,512]{2,1,0:T(8,128)(2,1)}, bf16[2,256,512]{2,1,0:T(8,128)(2,1)S(1)}, u32[]{:S(2)}, u32[]{:S(2)}) collective-permute-start(bf16[2,256,512]{2,1,0:T(8,128)(2,1)} %keys.1), channel_id=1, source_target_pairs={{0,4},{4,0},{8,12},{12,8},{16,20},{20,16},{24,28},{28,24},{32,36},... | collective-permute-start | bytes 1572872 | tf_op jit(solution)/shard_map/ppermute | solution.py:227
  23.0 4.4 %collective-permute-start.1 = (bf16[2,256,512]{2,1,0:T(8,128)(2,1)}, bf16[2,256,512]{2,1,0:T(8,128)(2,1)S(1)}, u32[]{:S(2)}, u32[]{:S(2)}) collective-permute-start(bf16[2,256,512]{2,1,0:T(8,128)(2,1)} %values.1), channel_id=1, source_target_pairs={{0,4},{4,0},{8,12},{12,8},{16,20},{20,16},{24,28},{28,24},{32,36},... | collective-permute-start | bytes 1572872 | tf_op jit(solution)/shard_map/ppermute | solution.py:227

commit v6 on v4

--- a/solution.py
+++ b/solution.py
@@ -67,7 +67,7 @@
     return mine, mine * live0, mine * live1
 
 
-def box_kernel(queries, shelf_ids, live_mask, box):
+def box_kernel(queries, shelf_ids, live_mask, box, built, sent):
     requests, width = queries.shape
     chips = box.shape[0]
     half = chips * SLOTS
@@ -82,8 +82,18 @@
         jnp.concatenate([(lane == n).astype(f32) for n in range(len(dead))], axis=0).astype(bf16),
         ((0,), (0,)),
     )
-    both = jnp.concatenate([rows[:half], rows[half:], flags], axis=1).astype(bf16)
-    box[...] = both.reshape(box.shape)
+    pieces = sent.shape[0]
+    part = chips // pieces
+    copies = []
+    for n in range(pieces):
+        own = slice(n * part * SLOTS, (n + 1) * part * SLOTS)
+        both = jnp.concatenate([rows[:half][own], rows[half:][own], flags[own]], axis=1)
+        at = pl.ds(n * part, part)
+        built[at] = both.astype(bf16).reshape(part, SLOTS, both.shape[1])
+        copies.append(pltpu.make_async_copy(built.at[at], box.at[at], sent.at[n]))
+        copies[-1].start()
+    for copy in copies:
+        copy.wait()
 
 
 def shelf_kernel(box, keys, values, other_keys, other_values, w_out, out, w_near, got, arrived):
@@ -170,7 +180,7 @@
         attended = jnp.where(head_of == h, part, attended)
     attended = attended.astype(bf16)
     groups, _, columns = out.shape
-    for n, g in enumerate(rotated(groups, groups // 2)):
+    for n, g in enumerate(rotated(groups, groups // 4)):
         out[n] = dot(attended, w_out[:, g * columns : (g + 1) * columns], ((1,), (0,)))
 
 
@@ -241,7 +251,15 @@
     wide = CORES * width + LANES
     box_array = ((chips, SLOTS, wide), bf16)
     rows = pltpu.VMEM((chips * SLOTS, wide), bf16)
-    (box,) = call(box_kernel, [box_array], "box", (), (queries, shelf_ids, live_mask))
+    box = pl.pallas_call(
+        box_kernel,
+        out_shape=jax.ShapeDtypeStruct(*box_array),
+        in_specs=[pl.BlockSpec(memory_space=pltpu.VMEM)] * 3,
+        out_specs=pl.BlockSpec(memory_space=pl.ANY),
+        scratch_shapes=[pltpu.VMEM(*box_array), pltpu.SemaphoreType.DMA((4,))],
+        compiler_params=pltpu.CompilerParams(vmem_limit_bytes=4 << 20),
+        name="box",
+    )(*[pltpu.with_memory_space_constraint(a, pltpu.HBM) for a in (queries, shelf_ids, live_mask)])
     keys, values, ids_near, live_near = staged(passage_keys, passage_values, shelf_ids, live_mask)
     partials, w_near = call(
         shelf_kernel,
@@ -264,7 +282,7 @@
         (exchanged(partials, "psg", same_core), w_near, ids_near, live_near),
         scratch=(rows,),
     )
-    blocks = exchanged(projected, "head", [rotated(groups, groups // 2)])
+    blocks = exchanged(projected, "head", [rotated(groups, groups // 4)])
     return jnp.sum(blocks, axis=0).astype(bf16)
 
 

time: 76.3 us -> 77.8 us (1.020)
  the two profiles are of different devices: /device:TPU:16 before, /device:TPU:4 now
where the time goes in v6:
time: 77.8 us; the launch traced here: 77.5 us
  blocking collectives  37.5 us (48%)
  starting transfers between devices  22.6 us (29%)
  waiting for transfers between devices  11.1 us (14%)
  Pallas kernels  5.62 us (7%)
    all_to_all x2, blocking collectives, exchanged(): lax.all_to_all(x, axis, split_axis=0, concat_axis=0, axis_index_groups=in...  37.5 us
    all_to_all x1, starting transfers between devices, exchanged(): lax.all_to_all(x, axis, split_axis=0, concat_axis=0, axis_index_groups=in...  18.3 us
    all_to_all x1, waiting for transfers between devices, exchanged(): lax.all_to_all(x, axis, split_axis=0, concat_axis=0, axis_index_groups=in...  10.6 us
    ppermute x2, starting transfers between devices, from_other_core(): return lax.ppermute(x, 'psg', [(i, i ^ 1) for i in range(owners)])  4.33 us
    pallas_call x2, Pallas kernels, call(): pl.pallas_call(kernel, out_shape=[in_vmem(*result) for result in results]...  2.5 us
    pallas_call x1, Pallas kernels, per_device(): pl.pallas_call(box_kernel, out_shape=jax.ShapeDtypeStruct(*box_array), in...  1.87 us
  transfers between devices with their start and end apart: 3, of which 2 were waited for; matrix products, arithmetic and copies ran while one was open for 0% of the time, Pallas kernels for 2%

profile of v6, /device:TPU:4, one launch (start us, length us, event | category | flops | bytes accessed | tf_op | source)
XLA Modules:
  0.0 77.5 jit_solution(9431627474384542380)
XLA Ops:
  0.0 1.9 %box.1 = bf16[64,2,1152]{2,1,0:T(2,128)(2,1)} custom-call(bf16[8,512]{1,0:T(8,128)(2,1)} %queries.1, s32[8,16]{1,0:T(8,128)} %refs_2_.1, s32[8,32]{1,0:T(8,128)} %refs_3_.1), custom_call_target="tpu_custom_call" | custom-call | tf_op jit(solution)/shard_map/box/pallas_call | solution.py:254
  1.9 18.3 %all-to-all-start = ((bf16[64,2,1152]{2,1,0:T(2,128)(2,1)}), bf16[64,2,1152]{2,1,0:T(2,128)(2,1)S(1)}, u32[]{:S(2)}, u32[]{:S(2)}) async-start(bf16[64,2,1152]{2,1,0:T(2,128)(2,1)} %box.1), calls=%async_computation | async-start | bytes 589824 | tf_op jit(solution)/shard_map/all_to_all | solution.py:242
  20.2 1.9 %collective-permute-start = (bf16[2,256,512]{2,1,0:T(8,128)(2,1)}, bf16[2,256,512]{2,1,0:T(8,128)(2,1)S(1)}, u32[]{:S(2)}, u32[]{:S(2)}) collective-permute-start(bf16[2,256,512]{2,1,0:T(8,128)(2,1)} %refs_0_.1), channel_id=1, source_target_pairs={{0,4},{4,0},{8,12},{12,8},{16,20},{20,16},{24,28},{28,24},{32,36},... | collective-permute-start | bytes 1572872 | tf_op jit(solution)/shard_map/ppermute | solution.py:247
  22.1 2.4 %collective-permute-start.1 = (bf16[2,256,512]{2,1,0:T(8,128)(2,1)}, bf16[2,256,512]{2,1,0:T(8,128)(2,1)S(1)}, u32[]{:S(2)}, u32[]{:S(2)}) collective-permute-start(bf16[2,256,512]{2,1,0:T(8,128)(2,1)} %refs_1_.1), channel_id=1, source_target_pairs={{0,4},{4,0},{8,12},{12,8},{16,20},{20,16},{24,28},{28,24},{32,36},... | collective-permute-start | bytes 1572872 | tf_op jit(solution)/shard_map/ppermute | solution.py:247
  24.5 1.2 %stage.1 = (bf16[2,256,512]{2,1,0:T(8,128)(2,1)S(1)}, bf16[2,256,512]{2,1,0:T(8,128)(2,1)S(1)}, s32[8,16]{1,0:T(8,128)S(1)}, s32[8,32]{1,0:T(8,128)S(1)}) custom-call(bf16[2,256,512]{2,1,0:T(8,128)(2,1)} %refs_0_.1, bf16[2,256,512]{2,1,0:T(8,128)(2,1)} %refs_1_.1, s32[8,16]{1,0:T(8,128)} %refs_2_.1, s32[8,32]{1,0:T(8,128)} %refs_3_.1), custom_call_target="tpu_custom_call" | custom-call | tf_op jit(solution)/shard_map/stage/pallas_call | solution.py:208
  25.8 0.0 collective-permute-done.other_keys
  25.8 0.5 collective-permute-done.1.other_values
  26.2 10.6 %all-to-all-done.box = bf16[64,2,1152]{2,1,0:T(2,128)(2,1)S(1)} async-done(((bf16[64,2,1152]{2,1,0:T(2,128)(2,1)}), bf16[64,2,1152]{2,1,0:T(2,128)(2,1)S(1)}, u32[]{:S(2)}, u32[]{:S(2)}) %all-to-all-start) | async-done | bytes 294944 | tf_op jit(solution)/shard_map/all_to_all | solution.py:242
  36.8 1.7 %shelf.1 = (bf16[64,2,1152]{2,1,0:T(2,128)(2,1)S(1)}, bf16[512,2048]{1,0:T(8,128)(2,1)S(1)}) custom-call(bf16[64,2,1152]{2,1,0:T(2,128)(2,1)S(1)} %all-to-all-done.box, bf16[2,256,512]{2,1,0:T(8,128)(2,1)S(1)} %get-tuple-element.11.keys, bf16[2,256,512]{2,1,0:T(8,128)(2,1)S(1)} %get-tuple-element.12.values, ...), custom_call_target="tpu_custom_call" | custom-call | tf_op jit(solution)/shard_map/shelf/pallas_call | solution.py:225
  38.6 28.0 %all_to_all.15.box = bf16[64,2,1152]{2,1,0:T(2,128)(2,1)S(1)} all-to-all(bf16[64,2,1152]{2,1,0:T(2,128)(2,1)S(1)} %get-tuple-element.13), channel_id=1, replica_groups={{360,368,376,384,392,400,408,416,424,432,440,448,456,464,472,480,488,49..., dimensions={0} | all-to-all | bytes 589824 | tf_op jit(solution)/shard_map/all_to_all | solution.py:242
  66.5 0.8 %merge.1 = f32[4,8,512]{2,1,0:T(8,128)S(1)} custom-call(bf16[64,2,1152]{2,1,0:T(2,128)(2,1)S(1)} %all_to_all.15.box, bf16[512,2048]{1,0:T(8,128)(2,1)S(1)} %get-tuple-element.14.w_out, s32[8,16]{1,0:T(8,128)S(1)} %get-tuple-element.15.shelf_ids, s32[8,32]{1,0:T(8,128)S(1)} %get-tuple-element.16.live_mask), custom_call_target="tpu_custom_call" | custom-call | tf_op jit(solution)/shard_map/merge/pallas_call | solution.py:225
  67.3 9.5 %all_to_all.16 = f32[4,8,512]{2,1,0:T(8,128)S(1)} all-to-all(f32[4,8,512]{2,1,0:T(8,128)S(1)} %merge.1), channel_id=1, replica_groups={{1,2,3,0},{5,6,7,4},{9,10,11,8},{13,14,15,12},{17,18,19,16},{21,22,23,2..., dimensions={0} | all-to-all | bytes 131072 | tf_op jit(solution)/shard_map/all_to_all | solution.py:242
  76.8 0.6 reduce_sum.9
Async XLA Ops:
  1.9 35.0 %all-to-all-start = ((bf16[64,2,1152]{2,1,0:T(2,128)(2,1)}), bf16[64,2,1152]{2,1,0:T(2,128)(2,1)S(1)}, u32[]{:S(2)}, u32[]{:S(2)}) async-start(bf16[64,2,1152]{2,1,0:T(2,128)(2,1)} %box.1), calls=%async_computation | async-start | bytes 589824 | tf_op jit(solution)/shard_map/all_to_all | solution.py:242
  20.2 5.6 %collective-permute-start = (bf16[2,256,512]{2,1,0:T(8,128)(2,1)}, bf16[2,256,512]{2,1,0:T(8,128)(2,1)S(1)}, u32[]{:S(2)}, u32[]{:S(2)}) collective-permute-start(bf16[2,256,512]{2,1,0:T(8,128)(2,1)} %refs_0_.1), channel_id=1, source_target_pairs={{0,4},{4,0},{8,12},{12,8},{16,20},{20,16},{24,28},{28,24},{32,36},... | collective-permute-start | bytes 1572872 | tf_op jit(solution)/shard_map/ppermute | solution.py:247
  22.1 4.1 %collective-permute-start.1 = (bf16[2,256,512]{2,1,0:T(8,128)(2,1)}, bf16[2,256,512]{2,1,0:T(8,128)(2,1)S(1)}, u32[]{:S(2)}, u32[]{:S(2)}) collective-permute-start(bf16[2,256,512]{2,1,0:T(8,128)(2,1)} %refs_1_.1), channel_id=1, source_target_pairs={{0,4},{4,0},{8,12},{12,8},{16,20},{20,16},{24,28},{28,24},{32,36},... | collective-permute-start | bytes 1572872 | tf_op jit(solution)/shard_map/ppermute | solution.py:247

commit v7 on v6

--- a/solution.py
+++ b/solution.py
@@ -180,7 +180,7 @@
         attended = jnp.where(head_of == h, part, attended)
     attended = attended.astype(bf16)
     groups, _, columns = out.shape
-    for n, g in enumerate(rotated(groups, groups // 4)):
+    for n, g in enumerate(rotated(groups, groups // 2)):
         out[n] = dot(attended, w_out[:, g * columns : (g + 1) * columns], ((1,), (0,)))
 
 
@@ -282,7 +282,7 @@
         (exchanged(partials, "psg", same_core), w_near, ids_near, live_near),
         scratch=(rows,),
     )
-    blocks = exchanged(projected, "head", [rotated(groups, groups // 4)])
+    blocks = exchanged(projected, "head", [rotated(groups, groups // 2)])
     return jnp.sum(blocks, axis=0).astype(bf16)
 
 

time: 77.8 us -> 76.4 us (0.982)
  the two profiles are of different devices: /device:TPU:4 before, /device:TPU:16 now
where the time goes in v7:
time: 76.4 us; the launch traced here: 76 us
  blocking collectives  36.1 us (47%)
  starting transfers between devices  23.5 us (31%)
  waiting for transfers between devices  10.2 us (13%)
  Pallas kernels  5.61 us (7%)
    all_to_all x2, blocking collectives, exchanged(): lax.all_to_all(x, axis, split_axis=0, concat_axis=0, axis_index_groups=in...  36.1 us
    all_to_all x1, starting transfers between devices, exchanged(): lax.all_to_all(x, axis, split_axis=0, concat_axis=0, axis_index_groups=in...  19.2 us
    all_to_all x1, waiting for transfers between devices, exchanged(): lax.all_to_all(x, axis, split_axis=0, concat_axis=0, axis_index_groups=in...  9.69 us
    ppermute x2, starting transfers between devices, from_other_core(): return lax.ppermute(x, 'psg', [(i, i ^ 1) for i in range(owners)])  4.33 us
    pallas_call x2, Pallas kernels, call(): pl.pallas_call(kernel, out_shape=[in_vmem(*result) for result in results]...  2.5 us
    pallas_call x1, Pallas kernels, per_device(): pl.pallas_call(box_kernel, out_shape=jax.ShapeDtypeStruct(*box_array), in...  1.87 us
  transfers between devices with their start and end apart: 3, of which 2 were waited for; matrix products, arithmetic and copies ran while one was open for 0% of the time, Pallas kernels for 2%

profile of v7, /device:TPU:16, one launch (start us, length us, event | category | flops | bytes accessed | tf_op | source)
XLA Modules:
  0.0 76.0 jit_solution(10990319754050077229)
XLA Ops:
  0.0 1.9 %box.1 = bf16[64,2,1152]{2,1,0:T(2,128)(2,1)} custom-call(bf16[8,512]{1,0:T(8,128)(2,1)} %queries.1, s32[8,16]{1,0:T(8,128)} %refs_2_.1, s32[8,32]{1,0:T(8,128)} %refs_3_.1), custom_call_target="tpu_custom_call" | custom-call | tf_op jit(solution)/shard_map/box/pallas_call | solution.py:254
  1.9 19.2 %all-to-all-start = ((bf16[64,2,1152]{2,1,0:T(2,128)(2,1)}), bf16[64,2,1152]{2,1,0:T(2,128)(2,1)S(1)}, u32[]{:S(2)}, u32[]{:S(2)}) async-start(bf16[64,2,1152]{2,1,0:T(2,128)(2,1)} %box.1), calls=%async_computation | async-start | bytes 589824 | tf_op jit(solution)/shard_map/all_to_all | solution.py:242
  21.1 1.9 %collective-permute-start = (bf16[2,256,512]{2,1,0:T(8,128)(2,1)}, bf16[2,256,512]{2,1,0:T(8,128)(2,1)S(1)}, u32[]{:S(2)}, u32[]{:S(2)}) collective-permute-start(bf16[2,256,512]{2,1,0:T(8,128)(2,1)} %refs_0_.1), channel_id=1, source_target_pairs={{0,4},{4,0},{8,12},{12,8},{16,20},{20,16},{24,28},{28,24},{32,36},... | collective-permute-start | bytes 1572872 | tf_op jit(solution)/shard_map/ppermute | solution.py:247
  23.0 2.4 %collective-permute-start.1 = (bf16[2,256,512]{2,1,0:T(8,128)(2,1)}, bf16[2,256,512]{2,1,0:T(8,128)(2,1)S(1)}, u32[]{:S(2)}, u32[]{:S(2)}) collective-permute-start(bf16[2,256,512]{2,1,0:T(8,128)(2,1)} %refs_1_.1), channel_id=1, source_target_pairs={{0,4},{4,0},{8,12},{12,8},{16,20},{20,16},{24,28},{28,24},{32,36},... | collective-permute-start | bytes 1572872 | tf_op jit(solution)/shard_map/ppermute | solution.py:247
  25.4 1.2 %stage.1 = (bf16[2,256,512]{2,1,0:T(8,128)(2,1)S(1)}, bf16[2,256,512]{2,1,0:T(8,128)(2,1)S(1)}, s32[8,16]{1,0:T(8,128)S(1)}, s32[8,32]{1,0:T(8,128)S(1)}) custom-call(bf16[2,256,512]{2,1,0:T(8,128)(2,1)} %refs_0_.1, bf16[2,256,512]{2,1,0:T(8,128)(2,1)} %refs_1_.1, s32[8,16]{1,0:T(8,128)} %refs_2_.1, s32[8,32]{1,0:T(8,128)} %refs_3_.1), custom_call_target="tpu_custom_call" | custom-call | tf_op jit(solution)/shard_map/stage/pallas_call | solution.py:208
  26.7 0.0 collective-permute-done.other_keys
  26.7 0.5 collective-permute-done.1.other_values
  27.2 9.7 %all-to-all-done.box = bf16[64,2,1152]{2,1,0:T(2,128)(2,1)S(1)} async-done(((bf16[64,2,1152]{2,1,0:T(2,128)(2,1)}), bf16[64,2,1152]{2,1,0:T(2,128)(2,1)S(1)}, u32[]{:S(2)}, u32[]{:S(2)}) %all-to-all-start) | async-done | bytes 294944 | tf_op jit(solution)/shard_map/all_to_all | solution.py:242
  36.9 1.7 %shelf.1 = (bf16[64,2,1152]{2,1,0:T(2,128)(2,1)S(1)}, bf16[512,2048]{1,0:T(8,128)(2,1)S(1)}) custom-call(bf16[64,2,1152]{2,1,0:T(2,128)(2,1)S(1)} %all-to-all-done.box, bf16[2,256,512]{2,1,0:T(8,128)(2,1)S(1)} %get-tuple-element.11.keys, bf16[2,256,512]{2,1,0:T(8,128)(2,1)S(1)} %get-tuple-element.12.values, ...), custom_call_target="tpu_custom_call" | custom-call | tf_op jit(solution)/shard_map/shelf/pallas_call | solution.py:225
  38.6 28.1 %all_to_all.15.box = bf16[64,2,1152]{2,1,0:T(2,128)(2,1)S(1)} all-to-all(bf16[64,2,1152]{2,1,0:T(2,128)(2,1)S(1)} %get-tuple-element.13), channel_id=1, replica_groups={{360,368,376,384,392,400,408,416,424,432,440,448,456,464,472,480,488,49..., dimensions={0} | all-to-all | bytes 589824 | tf_op jit(solution)/shard_map/all_to_all | solution.py:242
  66.7 0.8 %merge.1 = f32[4,8,512]{2,1,0:T(8,128)S(1)} custom-call(bf16[64,2,1152]{2,1,0:T(2,128)(2,1)S(1)} %all_to_all.15.box, bf16[512,2048]{1,0:T(8,128)(2,1)S(1)} %get-tuple-element.14.w_out, s32[8,16]{1,0:T(8,128)S(1)} %get-tuple-element.15.shelf_ids, s32[8,32]{1,0:T(8,128)S(1)} %get-tuple-element.16.live_mask), custom_call_target="tpu_custom_call" | custom-call | tf_op jit(solution)/shard_map/merge/pallas_call | solution.py:225
  67.4 8.0 %all_to_all.16 = f32[4,8,512]{2,1,0:T(8,128)S(1)} all-to-all(f32[4,8,512]{2,1,0:T(8,128)S(1)} %merge.1), channel_id=1, replica_groups={{2,3,0,1},{6,7,4,5},{10,11,8,9},{14,15,12,13},{18,19,16,17},{22,23,20,2..., dimensions={0} | all-to-all | bytes 131072 | tf_op jit(solution)/shard_map/all_to_all | solution.py:242
  75.4 0.6 reduce_sum.9
Async XLA Ops:
  1.9 35.0 %all-to-all-start = ((bf16[64,2,1152]{2,1,0:T(2,128)(2,1)}), bf16[64,2,1152]{2,1,0:T(2,128)(2,1)S(1)}, u32[]{:S(2)}, u32[]{:S(2)}) async-start(bf16[64,2,1152]{2,1,0:T(2,128)(2,1)} %box.1), calls=%async_computation | async-start | bytes 589824 | tf_op jit(solution)/shard_map/all_to_all | solution.py:242
  21.1 5.6 %collective-permute-start = (bf16[2,256,512]{2,1,0:T(8,128)(2,1)}, bf16[2,256,512]{2,1,0:T(8,128)(2,1)S(1)}, u32[]{:S(2)}, u32[]{:S(2)}) collective-permute-start(bf16[2,256,512]{2,1,0:T(8,128)(2,1)} %refs_0_.1), channel_id=1, source_target_pairs={{0,4},{4,0},{8,12},{12,8},{16,20},{20,16},{24,28},{28,24},{32,36},... | collective-permute-start | bytes 1572872 | tf_op jit(solution)/shard_map/ppermute | solution.py:247
  23.0 4.1 %collective-permute-start.1 = (bf16[2,256,512]{2,1,0:T(8,128)(2,1)}, bf16[2,256,512]{2,1,0:T(8,128)(2,1)S(1)}, u32[]{:S(2)}, u32[]{:S(2)}) collective-permute-start(bf16[2,256,512]{2,1,0:T(8,128)(2,1)} %refs_1_.1), channel_id=1, source_target_pairs={{0,4},{4,0},{8,12},{12,8},{16,20},{20,16},{24,28},{28,24},{32,36},... | collective-permute-start | bytes 1572872 | tf_op jit(solution)/shard_map/ppermute | solution.py:247
